TPU v7x, 256 devices: a whole 4x4x8 slice. The times are simulated.
256 devices in a mesh: gy: 8 (over y, x_hi), gx: 32 (over x_lo, z, core).
Axes of the slice: x: 4 (x_hi: 2, x_lo: 2; x = x_hi * 2 + x_lo), y: 4, z: 8, core: 2. Of those that a mesh axis runs over, the one named last changes fastest.
Arguments:
- u_field: float32 [8, 2048, 2048], P(None, 'gx', 'gy')
- v_field: float32 [8, 2048, 2048], P(None, 'gx', 'gy')
- w_field: float32 [8, 2048, 2048], P(None, 'gx', 'gy')
- sep_x: int32 [16], replicated, may hold values from 1 to 128, as said below
- sep_y: int32 [16], replicated, may hold values from 1 to 256, as said below
- sep_z: int32 [16], replicated, may hold values from 1 to 4
Outputs:
- correlation: float32 [3, 16], replicated
Inputs may be any that keep to these rules, and one draw needn't show every extreme that they name: `sep_x`: every separation along x lies in 1 to 128, and 128 is among them in every draw; repeats may occur. `sep_y`: every separation along y lies in 1 to 256, and 256 is among them in every draw; repeats may occur.
All inputs are finite; a program needn't handle non-finite values.
Results may differ from a plain program's by a relative error of at most 0.0003.
Values sent between devices are 32-bit elements; how exact they have to be, the bound alone decides.
No kernel may reach another device: no remote copies, remote signals or barrier semaphores. Data moves between devices by JAX's collectives and lax.ppermute only.
A program may use at most 64 MiB of HBM per device.

v0:
```python
import jax
import jax.numpy as jnp
from jax import lax
from jax.sharding import Mesh
from jax.sharding import PartitionSpec as P

GX = ("gx_0", "gx_1", "gx_2")
GY = ("gy_0", "gy_1")
GY_GX = ("gy_0", "gy_1", "gx_0", "gx_1", "gx_2")


def from_behind(value, axis, steps):
    count = lax.axis_size(axis)
    pairs = [(source, (source + steps) % count) for source in range(count)]
    return lax.ppermute(value, axis, pairs)


def by_axis(x, axes):
    for axis in axes:
        x = lax.psum(x, axis)
    return x


def lag_sums(widened, leading, lag_values, length, axis_dim):

    def one_lag(lag_entry):
        offset, lag_value = lag_entry
        head = lax.dynamic_slice_in_dim(widened, offset, length, axis_dim)
        tail = lax.dynamic_slice_in_dim(widened, offset + lag_value, length, axis_dim)
        return jnp.sum(head * tail)

    return lax.map(one_lag, (leading, lag_values))


def local(u_field, v_field, w_field, sep_x, sep_y, sep_z):
    planes, width_x, width_y = u_field.shape
    u_next = from_behind(u_field, GX, -1)
    u_after = from_behind(u_next, GX, -1)
    wide_x = jnp.concatenate([u_field, u_next, u_after], axis=1)
    v_next = from_behind(v_field, GY, -1)
    wide_y = jnp.concatenate([v_field, v_next], axis=2)
    offset_x = jnp.zeros_like(sep_x)
    offset_y = jnp.zeros_like(sep_y)
    sums_x = lag_sums(wide_x, offset_x, sep_x, width_x, 1)
    sums_y = lag_sums(wide_y, offset_y, sep_y, width_y, 2)
    padded = jnp.concatenate([w_field, jnp.zeros_like(w_field)], axis=0)

    def along_z(lag_value):
        shifted = lax.dynamic_slice_in_dim(padded, lag_value, planes, 0)
        return jnp.sum(w_field * shifted)

    sums_z = lax.map(along_z, sep_z)
    products = jnp.stack([sums_x, sums_y, sums_z], axis=0)
    squares = jnp.stack(
        [jnp.sum(u_field * u_field), jnp.sum(v_field * v_field), jnp.sum(w_field * w_field)]
    )
    totals, energy = (by_axis(products, GY_GX), by_axis(squares, GY_GX))
    factor = jnp.float32(planes) / (jnp.float32(planes) - sep_z.astype(jnp.float32))
    row_x = totals[0] / energy[0]
    row_y = totals[1] / energy[1]
    row_z = totals[2] / energy[2] * factor
    return jnp.stack([row_x, row_y, row_z], axis=0)


def solution(mesh):
    finer = Mesh(mesh.devices.reshape(4, 2, 2, 8, 2), ("gy_0", "gy_1", "gx_0", "gx_1", "gx_2"))
    placed = (P(None, GX, GY), P(None, GX, GY), P(None, GX, GY), P(), P(), P())
    return jax.shard_map(local, mesh=finer, in_specs=placed, out_specs=P(), check_vma=False)
```

profile of v0, /device:TPU:1, one launch (start us, length us, event | category | flops | bytes accessed | tf_op | source)
XLA Modules:
  0.0 266.0 jit_solution(17516855033638149033)
XLA Ops:
  0.0 3.2 %collective-permute-start = (f32[8,64,256]{2,1,0:T(8,128)}, f32[8,64,256]{2,1,0:T(8,128)S(1)}, u32[]{:S(2)}, u32[]{:S(2)}) collective-permute-start(f32[8,64,256]{2,1,0:T(8,128)} %param.12), channel_id=1, source_target_pairs={{0,31},{1,0},{2,1},{3,2},{4,3},{5,4},{6,5},{7,6},{8,7},{9,8},{10,9... | collective-permute-start | bytes 1572872 | tf_op jit(solution)/shard_map/ppermute | solution.py:15
  3.2 3.5 %collective-permute-start.2 = (f32[8,64,256]{2,1,0:T(8,128)}, f32[8,64,256]{2,1,0:T(8,128)}, u32[]{:S(2)}, u32[]{:S(2)}) collective-permute-start(f32[8,64,256]{2,1,0:T(8,128)} %param.13), channel_id=1, source_target_pairs={{0,224},{32,0},{64,32},{96,64},{128,96},{160,128},{192,160},{224,1... | collective-permute-start | bytes 1572872 | tf_op jit(solution)/shard_map/ppermute | solution.py:15
  6.7 1.1 concatenate.11
  7.9 69.8 %while.32 = (s32[]{:T(128)}, f32[16]{0:T(128)S(1)}, s32[16]{0:T(128)S(1)}, f32[16,64,256]{2,1,0:T(8,128)S(1)}, f32[8,64,256]{2,1,0:T(8,128)S(1)}, /*index=5*/s32[]{:T(128)}, s32[]{:T(128)}, s32[]{:T(128)}) while((s32[]{:T(128)}, f32[16]{0:T(128)S(1)}, s32[16]{0:T(128)S(1)}, f32[16,64,256]{2,1,0:T(8,128)S(1)}, f32[8,64,256]{2,1,0:T(8,128)S(1)}, ...), condition=%wide.region_8.9_spmd, body=%wide.region_6.8_spmd.sunk | while | flops 262148 | bytes 1048727 | solution.py:52
  80.1 2.0 pad_maximum_fusion.4
  82.0 6.2 %collective-permute-start.1 = (f32[8,64,256]{2,1,0:T(8,128)S(1)}, f32[8,64,256]{2,1,0:T(8,128)}, u32[]{:S(2)}, u32[]{:S(2)}) collective-permute-start(f32[8,64,256]{2,1,0:T(8,128)S(1)} %collective-permute-done), channel_id=1, source_target_pairs={{0,31},{1,0},{2,1},{3,2},{4,3},{5,4},{6,5},{7,6},{8,7},{9,8},{10,9... | collective-permute-start | bytes 1572872 | tf_op jit(solution)/shard_map/ppermute | solution.py:15
  88.3 1.2 pad_maximum_fusion.1
  89.5 70.8 %while.31 = (s32[]{:T(128)}, f32[16]{0:T(128)S(1)}, f32[8,64,512]{2,1,0:T(8,128)S(1)}, s32[16]{0:T(128)S(1)}, s32[]{:T(128)}, /*index=5*/s32[]{:T(128)}, s32[]{:T(128)}) while((s32[]{:T(128)}, f32[16]{0:T(128)S(1)}, f32[8,64,512]{2,1,0:T(8,128)S(1)}, s32[16]{0:T(128)S(1)}, s32[]{:T(128)}, /*index=5*/s32[]{:T(128)}, s32[]{:T(128)}) %tuple.58), condition=%wide.region_5.6_spmd, body=%wide.region_3.5_spmd.sunk | while | flops 262148 | bytes 1048719 | solution.py:32
  101.1 0.9 multiply_reduce_fusion.10
  105.5 0.9 multiply_reduce_fusion.10
  109.9 0.9 multiply_reduce_fusion.10
  118.8 0.9 multiply_reduce_fusion.10
  123.2 0.9 multiply_reduce_fusion.10
  127.6 0.9 multiply_reduce_fusion.10
  145.3 0.9 multiply_reduce_fusion.10
  158.6 0.9 multiply_reduce_fusion.10
  160.3 1.2 pad_maximum_fusion
  161.5 64.5 %while.30 = (s32[]{:T(128)}, f32[16]{0:T(128)S(1)}, f32[8,192,256]{2,1,0:T(8,128)S(1)}, s32[16]{0:T(128)S(1)}, s32[]{:T(128)}, /*index=5*/s32[]{:T(128)}, s32[]{:T(128)}) while((s32[]{:T(128)}, f32[16]{0:T(128)S(1)}, f32[8,192,256]{2,1,0:T(8,128)S(1)}, s32[16]{0:T(128)S(1)}, s32[]{:T(128)}, /*index=5*/s32[]{:T(128)}, s32[]{:T(128)}) %tuple.59), condition=%wide.region_2.3_spmd, body=%wide.region_0.2_spmd.sunk | while | flops 262148 | bytes 1048719 | solution.py:32
  226.0 6.5 %all-reduce.2 = (f32[3,16]{1,0:T(4,128)S(1)}, f32[3]{0:T(128)S(1)}) all-reduce(f32[3,16]{1,0:T(4,128)S(1)} %pad_maximum_fusion.2, f32[3]{0:T(128)S(1)} %pad_maximum_fusion.4), channel_id=1, replica_groups=mesh['gy_0'=4,'gy_1'=2,'gx_0'=2,'gx_1'=8,'gx_2'=2] {'gy_0'}, use_global_device_ids=true, to_apply=%region_9.10 | all-reduce | flops 51 | bytes 408 | tf_op jit(solution)/shard_map/psum | solution.py:20
  232.5 5.3 %all-reduce.5 = (f32[3,16]{1,0:T(4,128)S(1)}, f32[3]{0:T(128)S(1)}) all-reduce(f32[3,16]{1,0:T(4,128)S(1)} %get-tuple-element.107, f32[3]{0:T(128)S(1)} %get-tuple-element.108), channel_id=1, replica_groups=mesh['gy_0'=4,'gy_1'=2,'gx_0'=2,'gx_1'=8,'gx_2'=2] {'gy_1'}, use_global_device_ids=true, to_apply=%region_10.11 | all-reduce | flops 51 | bytes 408 | tf_op jit(solution)/shard_map/psum | solution.py:20
  237.8 3.8 %all-reduce.4 = (f32[3,16]{1,0:T(4,128)S(1)}, f32[3]{0:T(128)S(1)}) all-reduce(f32[3,16]{1,0:T(4,128)S(1)} %get-tuple-element.113, f32[3]{0:T(128)S(1)} %get-tuple-element.114), channel_id=1, replica_groups=mesh['gy_0'=4,'gy_1'=2,'gx_0'=2,'gx_1'=8,'gx_2'=2] {'gx_0'}, use_global_device_ids=true, to_apply=%region_11.12 | all-reduce | flops 51 | bytes 408 | tf_op jit(solution)/shard_map/psum | solution.py:20
  241.5 10.7 %all-reduce.1 = (f32[3,16]{1,0:T(4,128)S(1)}, f32[3]{0:T(128)S(1)}) all-reduce(f32[3,16]{1,0:T(4,128)S(1)} %get-tuple-element.111, f32[3]{0:T(128)S(1)} %get-tuple-element.112), channel_id=1, replica_groups=mesh['gy_0'=4,'gy_1'=2,'gx_0'=2,'gx_1'=8,'gx_2'=2] {'gx_1'}, use_global_device_ids=true, to_apply=%region_12.13 | all-reduce | flops 51 | bytes 408 | tf_op jit(solution)/shard_map/psum | solution.py:20
  252.3 10.6 %all-reduce.3 = (f32[3,16]{1,0:T(4,128)S(1)}, f32[3]{0:T(128)S(1)}) all-reduce(f32[3,16]{1,0:T(4,128)S(1)} %get-tuple-element.105, f32[3]{0:T(128)S(1)} %get-tuple-element.106), channel_id=1, replica_groups=mesh['gy_0'=4,'gy_1'=2,'gx_0'=2,'gx_1'=8,'gx_2'=2] {'gx_2'}, use_global_device_ids=true, to_apply=%region_13.14 | all-reduce | flops 51 | bytes 408 | tf_op jit(solution)/shard_map/psum | solution.py:20
  264.2 1.2 slice_divide_fusion.1
  (161 shorter events, 104.8 us)
Async XLA Ops:
  0.0 7.8 %copy-start = (f32[8,64,256]{2,1,0:T(8,128)S(1)}, f32[8,64,256]{2,1,0:T(8,128)}, u32[]{:S(2)}) copy-start(f32[8,64,256]{2,1,0:T(8,128)} %param.14) | copy-start | bytes 1572868
  0.0 7.8 %copy-start.3 = (s32[16]{0:T(128)S(1)}, s32[16]{0:T(128)}, u32[]{:S(2)}) copy-start(s32[16]{0:T(128)} %param.17) | copy-start | bytes 196
  0.0 82.0 %collective-permute-start = (f32[8,64,256]{2,1,0:T(8,128)}, f32[8,64,256]{2,1,0:T(8,128)S(1)}, u32[]{:S(2)}, u32[]{:S(2)}) collective-permute-start(f32[8,64,256]{2,1,0:T(8,128)} %param.12), channel_id=1, source_target_pairs={{0,31},{1,0},{2,1},{3,2},{4,3},{5,4},{6,5},{7,6},{8,7},{9,8},{10,9... | collective-permute-start | bytes 1572872 | tf_op jit(solution)/shard_map/ppermute | solution.py:15
  3.2 85.1 %collective-permute-start.2 = (f32[8,64,256]{2,1,0:T(8,128)}, f32[8,64,256]{2,1,0:T(8,128)}, u32[]{:S(2)}, u32[]{:S(2)}) collective-permute-start(f32[8,64,256]{2,1,0:T(8,128)} %param.13), channel_id=1, source_target_pairs={{0,224},{32,0},{64,32},{96,64},{128,96},{160,128},{192,160},{224,1... | collective-permute-start | bytes 1572872 | tf_op jit(solution)/shard_map/ppermute | solution.py:15
  7.9 69.9 %copy-start.1 = (f32[8,64,256]{2,1,0:T(8,128)S(1)}, f32[8,64,256]{2,1,0:T(8,128)}, u32[]{:S(2)}) copy-start(f32[8,64,256]{2,1,0:T(8,128)} %param.13) | copy-start | bytes 1572868
  7.9 71.4 %copy-start.2 = (f32[8,64,256]{2,1,0:T(8,128)S(1)}, f32[8,64,256]{2,1,0:T(8,128)}, u32[]{:S(2)}) copy-start(f32[8,64,256]{2,1,0:T(8,128)} %param.12) | copy-start | bytes 1572868
  78.4 11.0 %copy-start.4 = (s32[16]{0:T(128)S(1)}, s32[16]{0:T(128)}, u32[]{:S(2)}) copy-start(s32[16]{0:T(128)} %param.16) | copy-start | bytes 196
  82.0 78.3 %collective-permute-start.1 = (f32[8,64,256]{2,1,0:T(8,128)S(1)}, f32[8,64,256]{2,1,0:T(8,128)}, u32[]{:S(2)}, u32[]{:S(2)}) collective-permute-start(f32[8,64,256]{2,1,0:T(8,128)S(1)} %collective-permute-done), channel_id=1, source_target_pairs={{0,31},{1,0},{2,1},{3,2},{4,3},{5,4},{6,5},{7,6},{8,7},{9,8},{10,9... | collective-permute-start | bytes 1572872 | tf_op jit(solution)/shard_map/ppermute | solution.py:15
  160.3 1.2 copy-start.5
where the time goes:
time: 268 us; the launch traced here: 266 us
  loops' own time  97.6 us (36%)
  local copies, waits for them, and re-layouts  70.1 us (26%)
  other arithmetic  48.5 us (18%)
  blocking collectives  36.8 us (14%)
  starting transfers between devices  12.9 us (5%)
    another operation x2, loops' own time, lag_sums(): return lax.map(one_lag, (leading, lag_values))  64.4 us
    dynamic_update_slice x48, local copies, waits for them, and re-layouts, lag_sums(): return lax.map(one_lag, (leading, lag_values))  37.7 us
    psum x5, blocking collectives, by_axis(): x = lax.psum(x, axis)  36.8 us
    another operation x1, loops' own time, local(): sums_z = lax.map(along_z, sep_z)  33.3 us
    dynamic_slice x48, local copies, waits for them, and re-layouts, lag_sums(): return lax.map(one_lag, (leading, lag_values))  30.6 us
    reduce_sum x32, other arithmetic, one_lag(): return jnp.sum(head * tail)  26.2 us
    reduce_sum x16, other arithmetic, along_z(): return jnp.sum(w_field * shifted)  13.1 us
    ppermute x3, starting transfers between devices, from_behind(): return lax.ppermute(value, axis, pairs)  12.9 us
  transfers between devices with their start and end apart: 3, of which 0 were waited for; matrix products, arithmetic and copies ran while one was open for 30% of the time, Pallas kernels for 0%

commit v1 on v0

v1 whole, which is shorter than its diff:
```python
import functools

import jax
import jax.numpy as jnp
from jax import lax
from jax.experimental import pallas as pl
from jax.experimental.pallas import tpu as pltpu
from jax.sharding import Mesh
from jax.sharding import PartitionSpec as P

SHAPE = (4, 2, 2, 8, 2)
AXES = ("y", "xh", "xl", "z", "c")
GX = ("xl", "z", "c")
GY = ("y", "xh")
F32 = jnp.float32
HIGH = lax.Precision.HIGHEST


def pairs_of(target):
    def flat(at):
        index = 0
        for size, i in zip(SHAPE, at):
            index = index * size + i % size
        return index

    places = [()]
    for size in SHAPE:
        places = [at + (i,) for at in places for i in range(size)]
    return [(flat(at), flat(target(*at))) for at in places]


U_KEEP = pairs_of(lambda y, xh, xl, z, c: (y, xh, xl, z - 1 + 2 * c, c))
U_SEND = pairs_of(lambda y, xh, xl, z, c: (y, xh, xl, z + 1 - 2 * c, c))
CORES = pairs_of(lambda y, xh, xl, z, c: (y, xh, xl, z, 1 - c))


def wrapped(pairs_fn):
    return pairs_of(pairs_fn)


def u_target(step):
    def target(y, xh, xl, z, c):
        chip = (xl * 8 + z + step(c)) % 16
        return (y, xh, chip // 8, chip % 8, c)

    return target


U_KEEP = pairs_of(u_target(lambda c: -1 if c == 0 else 1))
U_SEND = pairs_of(u_target(lambda c: 1 if c == 0 else -1))
V_SWAP = pairs_of(lambda y, xh, xl, z, c: (y, 1 - xh, xl, z, c))
V_KEEP = pairs_of(lambda y, xh, xl, z, c: (y - 1 if xh == 0 else y + 1, xh, xl, z, c))


def dot_nt(a, b):
    return lax.dot_general(a, b, (((1,), (1,)), ((), ())), precision=HIGH, preferred_element_type=F32)


def dot_tn(a, b):
    return lax.dot_general(a, b, (((0,), (0,)), ((), ())), precision=HIGH, preferred_element_type=F32)


def lane_index():
    return lax.broadcasted_iota(jnp.int32, (8, 128), 1)


def row_index():
    return lax.broadcasted_iota(jnp.int32, (8, 128), 0)


def lag_row(refs):
    lane = lane_index()
    lags = jnp.zeros((8, 128), jnp.int32)
    for axis, ref in enumerate(refs):
        for k in range(16):
            lags = jnp.where(lane == axis * 16 + k, ref[k], lags)
    return lags


def skewed(gram):
    rows, lanes = gram.shape
    total = gram[:8]
    for i in range(8, rows, 8):
        total = total + pltpu.roll(gram[i : i + 8], (lanes - i) % lanes, 1)
    return total


def pick(skew, diagonal):
    lanes = skew.shape[1]
    at = (diagonal + row_index()) & (lanes - 1)
    got = jnp.zeros((8, 128), F32)
    for t in range(lanes // 128):
        part = jnp.take_along_axis(skew[:, t * 128 : (t + 1) * 128], at & 127, axis=1)
        got = jnp.where((at >> 7) == t, part, got)
    return jnp.broadcast_to(jnp.sum(got, axis=0, keepdims=True), (8, 128))


def widened(gram):
    return jnp.concatenate([gram, jnp.zeros(gram.shape, F32)], axis=1)


def own_kernel(sx, sy, sz, u_ref, v_ref, w_ref, out_ref):
    lags = lag_row((sx, sy, sz))
    lane = lane_index()
    u_gram = jnp.zeros((64, 128), F32)
    pad = jnp.zeros((64, 256), F32)
    for z in range(8):
        plane = u_ref[z]
        u_gram = u_gram + dot_nt(plane, jnp.concatenate([plane, pad], axis=0))
    u_sums = pick(skewed(u_gram), lags)
    u_sums = jnp.where(lags < 64, u_sums, 0.0)
    v_rows = v_ref[...].reshape(512, 256)
    v_sums = pick(skewed(widened(dot_tn(v_rows, v_rows))), lags)
    planes = [w_ref[z] for z in range(8)]
    w_sums = jnp.zeros((8, 128), F32)
    for lag in range(5):
        total = planes[0] * planes[lag]
        for z in range(1, 8 - lag):
            total = total + planes[z] * planes[z + lag]
        total = jnp.sum(jnp.sum(total, axis=0, keepdims=True), axis=1, keepdims=True)
        w_sums = jnp.where(lags == lag, total, w_sums)
    w_sums = w_sums * 8.0 / (8.0 - lags.astype(F32))
    of_u = (lane < 16) | (lane == 48)
    of_v = (lane < 32) | (lane == 49)
    out_ref[...] = jnp.where(of_u, u_sums, jnp.where(of_v, v_sums, w_sums))


def v_kernel(sx, sy, sz, own, other, near, before, out_ref):
    lags = lag_row((sx, sy, sz))
    lane = lane_index()
    first = lax.axis_index("xh") == 0
    a = own[...].reshape(256, 256)
    b = other[...].reshape(256, 256)
    c = near[...].reshape(256, 256)
    gram = dot_tn(a, b) + dot_tn(b, c)
    sums = pick(skewed(widened(gram)), jnp.where(first, lags - 256, 256 - lags))
    out_ref[...] = before[...] + jnp.where((lane >= 16) & (lane < 32), sums, 0.0)


def u_kernel(sx, sy, sz, keep, send, other, near_keep, near_send, before, out_ref):
    lags = lag_row((sx, sy, sz))
    lane = lane_index()
    first = lax.axis_index("c") == 0
    gram = jnp.zeros((64, 128), F32)
    pad = jnp.zeros((64, 256), F32)
    for z in range(4):
        a, b, c = keep[z], other[z], near_keep[z]
        gram = gram + dot_nt(a, jnp.concatenate([b, c], axis=0))
        gram = gram + dot_nt(b, jnp.concatenate([c, pad], axis=0))
        gram = gram + dot_nt(near_send[z], jnp.concatenate([pad, send[z]], axis=0))
    i = lax.broadcasted_iota(jnp.int32, (64, 128), 0)
    j = lax.broadcasted_iota(jnp.int32, (64, 128), 1) - 64
    ahead = jnp.where(first, i - j, j - i)
    gram = jnp.where((j < 0) | (ahead >= 0), gram, 0.0)
    sums = pick(skewed(gram), jnp.where(first, lags - 64, 64 - lags))
    out_ref[...] = before[...] + jnp.where(lane < 16, sums, 0.0)


def end_kernel(parts, out_ref):
    total = parts[0]
    for d in range(1, parts.shape[0]):
        total = total + parts[d]
    lane = lax.broadcasted_iota(jnp.int32, (1, 128), 1)
    for axis in range(3):
        energy = jnp.sum(jnp.where(lane == 48 + axis, total, 0.0), axis=1, keepdims=True)
        out_ref[axis : axis + 1, :] = total[:, axis * 16 : axis * 16 + 16] / energy


SMEM = pl.BlockSpec(memory_space=pltpu.SMEM)
VMEM = pl.BlockSpec(memory_space=pltpu.VMEM)


def call(kernel, shape, *args):
    specs = [SMEM if a.dtype == jnp.int32 else VMEM for a in args]
    return pl.pallas_call(
        kernel, out_shape=jax.ShapeDtypeStruct(shape, F32), in_specs=specs, out_specs=VMEM, name=kernel.__name__
    )(*args)


def local(u, v, w, sep_x, sep_y, sep_z):
    core = lax.axis_index("c")
    half = lax.axis_index("xh")
    u_keep = lax.dynamic_slice_in_dim(u, 4 * core, 4, 0)
    u_send = lax.dynamic_slice_in_dim(u, 4 - 4 * core, 4, 0)
    v_keep = lax.dynamic_slice_in_dim(v, 4 * half, 4, 0)
    v_send = lax.dynamic_slice_in_dim(v, 4 - 4 * half, 4, 0)
    v_other = lax.ppermute(v_send, AXES, V_SWAP)
    v_near = lax.ppermute(v_keep, AXES, V_KEEP)
    near_keep = lax.ppermute(u_keep, AXES, U_KEEP)
    near_send = lax.ppermute(u_send, AXES, U_SEND)
    u_other = lax.ppermute(u_send, AXES, CORES)
    seps = (sep_x, sep_y, sep_z)
    part = call(own_kernel, (8, 128), *seps, u, v, w)
    part = call(v_kernel, (8, 128), *seps, v_keep, v_other, v_near, part)
    part = call(u_kernel, (8, 128), *seps, u_keep, u_send, u_other, near_keep, near_send, part)
    rows = lax.all_to_all(jnp.broadcast_to(part[:1], (256, 128)), AXES, 0, 0, tiled=True)
    return call(end_kernel, (3, 16), rows.reshape(256, 1, 128))


def solution(mesh):
    finer = Mesh(mesh.devices.reshape(SHAPE), AXES)
    placed = (P(None, GX, GY),) * 3 + (P(),) * 3
    return jax.shard_map(local, mesh=finer, in_specs=placed, out_specs=P(), check_vma=False)
```

time: 268 us -> 56.1 us (0.21)
  loops' own time: 97.6 us -> 0 us
  local copies, waits for them, and re-layouts: 70.1 us -> 4.81 us
  other arithmetic: 48.5 us -> 0 us
  Pallas kernels: 0 us -> 11.1 us
  blocking collectives: 36.8 us -> 27.9 us
    another operation x3 -> x0, loops' own time: 97.6 us -> none  [the longest x2 64.4 us: lag_sums(): return lax.map(one_lag, (leading, lag_values))]
    reduce_sum x51 -> x0, other arithmetic: 41.7 us -> none  [the longest x32 26.2 us: one_lag(): return jnp.sum(head * tail)]
    dynamic_update_slice x48 -> x0, local copies, waits for them, and re-layouts: 37.7 us -> none  [lag_sums(): return lax.map(one_lag, (leading, lag_values))]
    psum x5 -> x0, blocking collectives: 36.8 us -> none  [by_axis(): x = lax.psum(x, axis)]
    dynamic_slice x48 -> x2, local copies, waits for them, and re-layouts: 30.6 us -> 1.16 us  [the longest x1 1.13 us: local(): v_send = lax.dynamic_slice_in_dim(v, 4 - 4 * half, 4, 0)]
    all_to_all x0 -> x1, blocking collectives: none -> 27.9 us  [local(): lax.all_to_all(jnp.broadcast_to(part[:1], (256, 128)), AXES, 0, 0, tiled=...]
    pallas_call x0 -> x4, Pallas kernels: none -> 11.1 us  [call(): pl.pallas_call(kernel, out_shape=jax.ShapeDtypeStruct(shape, F32), in_spe...]
    another operation x4 -> x0, other arithmetic: 3.26 us -> none  [the longest x1 1.96 us: local(): jnp.stack([jnp.sum(u_field * u_field), jnp.sum(v_field * v_field), jnp.su...]
  transfers between devices with their start and end apart: 3 -> 5, of which waited for: 0 -> 1; matrix products, arithmetic and copies ran while one was open for 30% -> 0% of each run, Pallas kernels for 0% -> 10%
where the time goes in v1:
time: 56.1 us; the launch traced here: 55.8 us
  blocking collectives  27.9 us (50%)
  starting transfers between devices  11.9 us (21%)
  Pallas kernels  11.1 us (20%)
  local copies, waits for them, and re-layouts  4.81 us (9%)
    all_to_all x1, blocking collectives, local(): lax.all_to_all(jnp.broadcast_to(part[:1], (256, 128)), AXES, 0, 0, tiled=...  27.9 us
    pallas_call x4, Pallas kernels, call(): pl.pallas_call(kernel, out_shape=jax.ShapeDtypeStruct(shape, F32), in_spe...  11.1 us
    ppermute x1, starting transfers between devices, local(): near_send = lax.ppermute(u_send, AXES, U_SEND)  5.6 us
    ppermute x1, starting transfers between devices, local(): v_near = lax.ppermute(v_keep, AXES, V_KEEP)  3.63 us
    unnamed x18, local copies, waits for them, and re-layouts  2.89 us
    ppermute x1, starting transfers between devices, local(): u_other = lax.ppermute(u_send, AXES, CORES)  1.32 us
    ppermute x1, starting transfers between devices, local(): v_other = lax.ppermute(v_send, AXES, V_SWAP)  1.31 us
    dynamic_slice x1, local copies, waits for them, and re-layouts, local(): v_send = lax.dynamic_slice_in_dim(v, 4 - 4 * half, 4, 0)  1.13 us
  transfers between devices with their start and end apart: 5, of which 1 were waited for; matrix products, arithmetic and copies ran while one was open for 0% of the time, Pallas kernels for 10%

profile of v1, /device:TPU:1, one launch (start us, length us, event | category | flops | bytes accessed | tf_op | source)
XLA Modules:
  0.0 55.8 jit_solution(5126496349822986847)
XLA Ops:
  0.0 1.1 %constant_dynamic-slice_fusion = (f32[4,64,256]{2,1,0:T(8,128)S(1)}, f32[4,64,256]{2,1,0:T(8,128)S(1)}) fusion(f32[8,64,256]{2,1,0:T(8,128)} %v_ref.1, s32[]{:T(128)S(6)} %select_n.15, s32[]{:T(128)S(6)} %select_n.14), kind=kLoop, calls=%fused_computation | loop fusion | bytes 1048584 | tf_op jit(solution)/shard_map/dynamic_slice | solution.py:186
  1.1 0.0 copy-start.1
  1.1 3.6 %collective-permute-start.4 = (f32[4,64,256]{2,1,0:T(8,128)S(1)}, f32[4,64,256]{2,1,0:T(8,128)S(1)}, u32[]{:S(2)}, u32[]{:S(2)}) collective-permute-start(f32[4,64,256]{2,1,0:T(8,128)S(1)} %get-tuple-element.6.own), channel_id=1, source_target_pairs={{0,192},{1,193},{2,194},{3,195},{4,196},{5,197},{6,198},{7,199},{8... | collective-permute-start | bytes 786440 | tf_op jit(solution)/shard_map/ppermute | solution.py:188
  4.8 1.3 %collective-permute-start.3 = (f32[4,64,256]{2,1,0:T(8,128)S(1)}, f32[4,64,256]{2,1,0:T(8,128)S(1)}, u32[]{:S(2)}, u32[]{:S(2)}) collective-permute-start(f32[4,64,256]{2,1,0:T(8,128)S(1)} %get-tuple-element.5), channel_id=1, source_target_pairs={{0,32},{1,33},{2,34},{3,35},{4,36},{5,37},{6,38},{7,39},{8,40},{9,... | collective-permute-start | bytes 786440 | tf_op jit(solution)/shard_map/ppermute | solution.py:187
  6.2 1.3 %collective-permute-start = (f32[4,64,256]{2,1,0:T(8,128)S(1)}, f32[4,64,256]{2,1,0:T(8,128)S(1)}, u32[]{:S(2)}, u32[]{:S(2)}) collective-permute-start(f32[4,64,256]{2,1,0:T(8,128)S(1)} %get-tuple-element.7.send), channel_id=1, source_target_pairs={{0,1},{1,0},{2,3},{3,2},{4,5},{5,4},{6,7},{7,6},{8,9},{9,8},{10,11... | collective-permute-start | bytes 786440 | tf_op jit(solution)/shard_map/ppermute | solution.py:191
  7.5 5.6 %collective-permute-start.2 = (f32[4,64,256]{2,1,0:T(8,128)S(1)}, f32[4,64,256]{2,1,0:T(8,128)S(1)}, u32[]{:S(2)}, u32[]{:S(2)}) collective-permute-start(f32[4,64,256]{2,1,0:T(8,128)S(1)} %get-tuple-element.7.send), channel_id=1, source_target_pairs={{0,2},{1,31},{2,4},{3,1},{4,6},{5,3},{6,8},{7,5},{8,10},{9,7},{10,... | collective-permute-start | bytes 786440 | tf_op jit(solution)/shard_map/ppermute | solution.py:190
  13.1 0.0 collective-permute-start.1
  13.1 3.2 %own_kernel.1.before = f32[8,128]{1,0:T(8,128)} custom-call(s32[16]{0:T(128)} %sx.5, s32[16]{0:T(128)} %sy.5, s32[16]{0:T(128)} %sz.5, f32[8,64,256]{2,1,0:T(8,128)} %u_ref.1, f32[8,64,256]{2,1,0:T(8,128)} %v_ref.1, f32[8,64,256]{2,1,0:T(8,128)} %w_ref.1), custom_call_target="tpu_custom_call" | custom-call | tf_op jit(solution)/shard_map/own_kernel/pallas_call | solution.py:175
  16.3 0.0 collective-permute-done.4.near
  16.3 0.0 collective-permute-done.3.other
  16.3 0.7 %copy-done.4 = f32[4,64,256]{2,1,0:T(8,128)} copy-done((f32[4,64,256]{2,1,0:T(8,128)}, f32[4,64,256]{2,1,0:T(8,128)S(1)}, u32[]{:S(2)}) %copy-start.4) | copy-done | bytes 262168
  17.0 0.7 %copy-done.5 = f32[4,64,256]{2,1,0:T(8,128)} copy-done((f32[4,64,256]{2,1,0:T(8,128)}, f32[4,64,256]{2,1,0:T(8,128)S(1)}, u32[]{:S(2)}) %copy-start.5) | copy-done | bytes 262168
  17.8 2.6 %v_kernel.1.before = f32[8,128]{1,0:T(8,128)} custom-call(s32[16]{0:T(128)} %sx.5, s32[16]{0:T(128)} %sy.5, s32[16]{0:T(128)} %sz.5, f32[4,64,256]{2,1,0:T(8,128)} %copy-done.1, f32[4,64,256]{2,1,0:T(8,128)} %copy-done.5, f32[4,64,256]{2,1,0:T(8,128)} %copy-done.4, f32[8,128]{1,0:T(8,128)} %own_kernel.1.before), custom_call_target="tpu_custom_call" | custom-call | tf_op jit(solution)/shard_map/v_kernel/pallas_call | solution.py:175
  20.3 0.0 collective-permute-done.other
  20.3 0.0 collective-permute-done.2.near_send
  20.3 0.1 collective-permute-done.1.near_keep
  20.4 0.6 %copy-done.6 = f32[4,64,256]{2,1,0:T(8,128)} copy-done((f32[4,64,256]{2,1,0:T(8,128)}, f32[4,64,256]{2,1,0:T(8,128)S(1)}, u32[]{:S(2)}) %copy-start.6) | copy-done | bytes 262168
  21.0 0.1 copy-done.7
  21.2 0.7 %copy-done.8 = f32[4,64,256]{2,1,0:T(8,128)} copy-done((f32[4,64,256]{2,1,0:T(8,128)}, f32[4,64,256]{2,1,0:T(8,128)S(1)}, u32[]{:S(2)}) %copy-start.8) | copy-done | bytes 262168
  21.9 3.4 %u_kernel.1 = f32[8,128]{1,0:T(8,128)} custom-call(s32[16]{0:T(128)} %sx.5, s32[16]{0:T(128)} %sy.5, s32[16]{0:T(128)} %sz.5, f32[4,64,256]{2,1,0:T(8,128)} %copy-done.3, f32[4,64,256]{2,1,0:T(8,128)} %copy-done.2, f32[4,64,256]{2,1,0:T(8,128)} %copy-done.6, f32[4,64,256]{2,1,0:T(8,128)} %copy-done.8, f32[4,64,256]{2,1,0:T(8,128)} %copy-done.7, ...), custom_call_target="tpu_custom_call" | custom-call | tf_op jit(solution)/shard_map/u_kernel/pallas_call | solution.py:175
  25.3 0.7 %slice_bitcast_fusion = f32[128]{0:T(128)S(1)} fusion(f32[8,128]{1,0:T(8,128)} %u_kernel.1), kind=kLoop, calls=%fused_computation.4 | loop fusion | bytes 1024 | tf_op jit(solution)/shard_map/slice | solution.py:196
  26.0 0.1 broadcast_in_dim.2
  26.0 27.9 %all_to_all.6.parts = f32[256,1,128]{2,1,0:T(1,128)} all-to-all(f32[256,1,128]{2,1,0:T(1,128)S(1)} %broadcast_in_dim.2), channel_id=1, replica_groups=mesh['y'=4,'xh'=2,'xl'=2,'z'=8,'c'=2] {'y','xh','xl','z','c'}, dimensions={0} | all-to-all | bytes 262144 | tf_op jit(solution)/shard_map/all_to_all | solution.py:196
  53.9 1.9 %end_kernel.1 = f32[3,16]{1,0:T(4,128)} custom-call(f32[256,1,128]{2,1,0:T(1,128)} %all_to_all.6.parts), custom_call_target="tpu_custom_call" | custom-call | tf_op jit(solution)/shard_map/end_kernel/pallas_call | solution.py:175
  (13 shorter events, 0.1 us)
Async XLA Ops:
  0.0 6.1 %copy-start = (f32[8,64,256]{2,1,0:T(8,128)S(1)}, f32[8,64,256]{2,1,0:T(8,128)}, u32[]{:S(2)}) copy-start(f32[8,64,256]{2,1,0:T(8,128)} %u_ref.1) | copy-start | bytes 1572868
  1.1 5.0 %copy-start.1 = (f32[4,64,256]{2,1,0:T(8,128)}, f32[4,64,256]{2,1,0:T(8,128)S(1)}, u32[]{:S(2)}) copy-start(f32[4,64,256]{2,1,0:T(8,128)S(1)} %get-tuple-element.6.own) | copy-start | bytes 786436
  1.1 15.2 %collective-permute-start.4 = (f32[4,64,256]{2,1,0:T(8,128)S(1)}, f32[4,64,256]{2,1,0:T(8,128)S(1)}, u32[]{:S(2)}, u32[]{:S(2)}) collective-permute-start(f32[4,64,256]{2,1,0:T(8,128)S(1)} %get-tuple-element.6.own), channel_id=1, source_target_pairs={{0,192},{1,193},{2,194},{3,195},{4,196},{5,197},{6,198},{7,199},{8... | collective-permute-start | bytes 786440 | tf_op jit(solution)/shard_map/ppermute | solution.py:188
  4.8 11.5 %collective-permute-start.3 = (f32[4,64,256]{2,1,0:T(8,128)S(1)}, f32[4,64,256]{2,1,0:T(8,128)S(1)}, u32[]{:S(2)}, u32[]{:S(2)}) collective-permute-start(f32[4,64,256]{2,1,0:T(8,128)S(1)} %get-tuple-element.5), channel_id=1, source_target_pairs={{0,32},{1,33},{2,34},{3,35},{4,36},{5,37},{6,38},{7,39},{8,40},{9,... | collective-permute-start | bytes 786440 | tf_op jit(solution)/shard_map/ppermute | solution.py:187
  6.1 10.2 %copy-start.2 = (f32[4,64,256]{2,1,0:T(8,128)}, f32[4,64,256]{2,1,0:T(8,128)S(1)}, u32[]{:S(2)}) copy-start(f32[4,64,256]{2,1,0:T(8,128)S(1)} %get-tuple-element.7.send) | copy-start | bytes 786436
  6.1 10.2 %copy-start.3 = (f32[4,64,256]{2,1,0:T(8,128)}, f32[4,64,256]{2,1,0:T(8,128)S(1)}, u32[]{:S(2)}) copy-start(f32[4,64,256]{2,1,0:T(8,128)S(1)} %get-tuple-element.8.keep) | copy-start | bytes 786436
  6.2 14.2 %collective-permute-start = (f32[4,64,256]{2,1,0:T(8,128)S(1)}, f32[4,64,256]{2,1,0:T(8,128)S(1)}, u32[]{:S(2)}, u32[]{:S(2)}) collective-permute-start(f32[4,64,256]{2,1,0:T(8,128)S(1)} %get-tuple-element.7.send), channel_id=1, source_target_pairs={{0,1},{1,0},{2,3},{3,2},{4,5},{5,4},{6,7},{7,6},{8,9},{9,8},{10,11... | collective-permute-start | bytes 786440 | tf_op jit(solution)/shard_map/ppermute | solution.py:191
  7.5 12.9 %collective-permute-start.2 = (f32[4,64,256]{2,1,0:T(8,128)S(1)}, f32[4,64,256]{2,1,0:T(8,128)S(1)}, u32[]{:S(2)}, u32[]{:S(2)}) collective-permute-start(f32[4,64,256]{2,1,0:T(8,128)S(1)} %get-tuple-element.7.send), channel_id=1, source_target_pairs={{0,2},{1,31},{2,4},{3,1},{4,6},{5,3},{6,8},{7,5},{8,10},{9,7},{10,... | collective-permute-start | bytes 786440 | tf_op jit(solution)/shard_map/ppermute | solution.py:190
  13.1 7.3 %collective-permute-start.1 = (f32[4,64,256]{2,1,0:T(8,128)S(1)}, f32[4,64,256]{2,1,0:T(8,128)S(1)}, u32[]{:S(2)}, u32[]{:S(2)}) collective-permute-start(f32[4,64,256]{2,1,0:T(8,128)S(1)} %get-tuple-element.8.keep), channel_id=1, source_target_pairs={{0,30},{1,3},{2,0},{3,5},{4,2},{5,7},{6,4},{7,9},{8,6},{9,11},{10,... | collective-permute-start | bytes 786440 | tf_op jit(solution)/shard_map/ppermute | solution.py:189
  16.3 0.7 %copy-start.4 = (f32[4,64,256]{2,1,0:T(8,128)}, f32[4,64,256]{2,1,0:T(8,128)S(1)}, u32[]{:S(2)}) copy-start(f32[4,64,256]{2,1,0:T(8,128)S(1)} %collective-permute-done.4.near) | copy-start | bytes 786436
  17.0 0.7 %copy-start.5 = (f32[4,64,256]{2,1,0:T(8,128)}, f32[4,64,256]{2,1,0:T(8,128)S(1)}, u32[]{:S(2)}) copy-start(f32[4,64,256]{2,1,0:T(8,128)S(1)} %collective-permute-done.3.other) | copy-start | bytes 786436
  20.3 0.7 %copy-start.6 = (f32[4,64,256]{2,1,0:T(8,128)}, f32[4,64,256]{2,1,0:T(8,128)S(1)}, u32[]{:S(2)}) copy-start(f32[4,64,256]{2,1,0:T(8,128)S(1)} %collective-permute-done.other) | copy-start | bytes 786436
  20.3 0.8 %copy-start.7 = (f32[4,64,256]{2,1,0:T(8,128)}, f32[4,64,256]{2,1,0:T(8,128)S(1)}, u32[]{:S(2)}) copy-start(f32[4,64,256]{2,1,0:T(8,128)S(1)} %collective-permute-done.2.near_send) | copy-start | bytes 786436
  21.1 0.7 %copy-start.8 = (f32[4,64,256]{2,1,0:T(8,128)}, f32[4,64,256]{2,1,0:T(8,128)S(1)}, u32[]{:S(2)}) copy-start(f32[4,64,256]{2,1,0:T(8,128)S(1)} %collective-permute-done.1.near_keep) | copy-start | bytes 786436

commit v2 on v1

--- a/solution.py
+++ b/solution.py
@@ -1,5 +1,3 @@
-import functools
-
 import jax
 import jax.numpy as jnp
 from jax import lax
@@ -8,6 +6,7 @@
 from jax.sharding import Mesh
 from jax.sharding import PartitionSpec as P
 
+
 SHAPE = (4, 2, 2, 8, 2)
 AXES = ("y", "xh", "xl", "z", "c")
 GX = ("xl", "z", "c")
@@ -29,15 +28,6 @@
     return [(flat(at), flat(target(*at))) for at in places]
 
 
-U_KEEP = pairs_of(lambda y, xh, xl, z, c: (y, xh, xl, z - 1 + 2 * c, c))
-U_SEND = pairs_of(lambda y, xh, xl, z, c: (y, xh, xl, z + 1 - 2 * c, c))
-CORES = pairs_of(lambda y, xh, xl, z, c: (y, xh, xl, z, 1 - c))
-
-
-def wrapped(pairs_fn):
-    return pairs_of(pairs_fn)
-
-
 def u_target(step):
     def target(y, xh, xl, z, c):
         chip = (xl * 8 + z + step(c)) % 16
@@ -48,6 +38,7 @@
 
 U_KEEP = pairs_of(u_target(lambda c: -1 if c == 0 else 1))
 U_SEND = pairs_of(u_target(lambda c: 1 if c == 0 else -1))
+CORES = pairs_of(lambda y, xh, xl, z, c: (y, xh, xl, z, 1 - c))
 V_SWAP = pairs_of(lambda y, xh, xl, z, c: (y, 1 - xh, xl, z, c))
 V_KEEP = pairs_of(lambda y, xh, xl, z, c: (y - 1 if xh == 0 else y + 1, xh, xl, z, c))
 
@@ -125,29 +116,36 @@
     out_ref[...] = jnp.where(of_u, u_sums, jnp.where(of_v, v_sums, w_sums))
 
 
-def v_kernel(sx, sy, sz, own, other, near, before, out_ref):
+def swap_kernel(own, other, out_ref):
+    gram = dot_tn(own[...].reshape(256, 256), other[...].reshape(256, 256))
+    out_ref[...] = skewed(widened(gram))
+
+
+def last_kernel(sx, sy, sz, other, near, skew, before, out_ref):
     lags = lag_row((sx, sy, sz))
     lane = lane_index()
     first = lax.axis_index("xh") == 0
-    a = own[...].reshape(256, 256)
-    b = other[...].reshape(256, 256)
-    c = near[...].reshape(256, 256)
-    gram = dot_tn(a, b) + dot_tn(b, c)
-    sums = pick(skewed(widened(gram)), jnp.where(first, lags - 256, 256 - lags))
-    out_ref[...] = before[...] + jnp.where((lane >= 16) & (lane < 32), sums, 0.0)
+    gram = dot_tn(other[...].reshape(256, 256), near[...].reshape(256, 256))
+    total = skew[...] + skewed(widened(gram))
+    sums = pick(total, jnp.where(first, lags - 256, 256 - lags))
+    row = before[...] + jnp.where((lane >= 16) & (lane < 32), sums, 0.0)
+    for i in range(0, out_ref.shape[0], 8):
+        out_ref[i : i + 8] = row
 
 
 def u_kernel(sx, sy, sz, keep, send, other, near_keep, near_send, before, out_ref):
     lags = lag_row((sx, sy, sz))
     lane = lane_index()
     first = lax.axis_index("c") == 0
-    gram = jnp.zeros((64, 128), F32)
-    pad = jnp.zeros((64, 256), F32)
+    left = jnp.zeros((64, 128), F32)
+    right = jnp.zeros((64, 64), F32)
+    pad = jnp.zeros((64, 64), F32)
     for z in range(4):
         a, b, c = keep[z], other[z], near_keep[z]
-        gram = gram + dot_nt(a, jnp.concatenate([b, c], axis=0))
-        gram = gram + dot_nt(b, jnp.concatenate([c, pad], axis=0))
-        gram = gram + dot_nt(near_send[z], jnp.concatenate([pad, send[z]], axis=0))
+        both = dot_nt(jnp.concatenate([a, b], axis=0), jnp.concatenate([b, c], axis=0))
+        left = left + both[:64] + jnp.concatenate([both[64:, 64:], pad], axis=1)
+        right = right + dot_nt(near_send[z], send[z])
+    gram = left + jnp.concatenate([pad, right], axis=1)
     i = lax.broadcasted_iota(jnp.int32, (64, 128), 0)
     j = lax.broadcasted_iota(jnp.int32, (64, 128), 1) - 64
     ahead = jnp.where(first, i - j, j - i)
@@ -157,9 +155,7 @@
 
 
 def end_kernel(parts, out_ref):
-    total = parts[0]
-    for d in range(1, parts.shape[0]):
-        total = total + parts[d]
+    total = jnp.sum(parts[...], axis=0, keepdims=True)
     lane = lax.broadcasted_iota(jnp.int32, (1, 128), 1)
     for axis in range(3):
         energy = jnp.sum(jnp.where(lane == 48 + axis, total, 0.0), axis=1, keepdims=True)
@@ -170,11 +166,17 @@
 VMEM = pl.BlockSpec(memory_space=pltpu.VMEM)
 
 
-def call(kernel, shape, *args):
+def call(kernel, out, *args):
     specs = [SMEM if a.dtype == jnp.int32 else VMEM for a in args]
-    return pl.pallas_call(
-        kernel, out_shape=jax.ShapeDtypeStruct(shape, F32), in_specs=specs, out_specs=VMEM, name=kernel.__name__
-    )(*args)
+    return pl.pallas_call(kernel, out_shape=out, in_specs=specs, out_specs=VMEM)(*args)
+
+
+def near(x):
+    return pltpu.with_memory_space_constraint(x, pltpu.VMEM)
+
+
+def send(value, pairs):
+    return near(lax.ppermute(value, AXES, pairs))
 
 
 def local(u, v, w, sep_x, sep_y, sep_z):
@@ -184,17 +186,19 @@
     u_send = lax.dynamic_slice_in_dim(u, 4 - 4 * core, 4, 0)
     v_keep = lax.dynamic_slice_in_dim(v, 4 * half, 4, 0)
     v_send = lax.dynamic_slice_in_dim(v, 4 - 4 * half, 4, 0)
-    v_other = lax.ppermute(v_send, AXES, V_SWAP)
-    v_near = lax.ppermute(v_keep, AXES, V_KEEP)
-    near_keep = lax.ppermute(u_keep, AXES, U_KEEP)
-    near_send = lax.ppermute(u_send, AXES, U_SEND)
-    u_other = lax.ppermute(u_send, AXES, CORES)
+    v_other = send(v_send, V_SWAP)
+    u_other = send(u_send, CORES)
+    near_keep = send(u_keep, U_KEEP)
+    near_send = send(u_send, U_SEND)
+    v_near = send(v_keep, V_KEEP)
     seps = (sep_x, sep_y, sep_z)
-    part = call(own_kernel, (8, 128), *seps, u, v, w)
-    part = call(v_kernel, (8, 128), *seps, v_keep, v_other, v_near, part)
-    part = call(u_kernel, (8, 128), *seps, u_keep, u_send, u_other, near_keep, near_send, part)
-    rows = lax.all_to_all(jnp.broadcast_to(part[:1], (256, 128)), AXES, 0, 0, tiled=True)
-    return call(end_kernel, (3, 16), rows.reshape(256, 1, 128))
+    row = pltpu.VMEM((8, 128), F32)
+    part = call(own_kernel, row, *seps, u, v, w)
+    skew = call(swap_kernel, pltpu.VMEM((8, 512), F32), near(v_keep), v_other)
+    part = call(u_kernel, row, *seps, near(u_keep), near(u_send), u_other, near_keep, near_send, near(part))
+    rows = call(last_kernel, pltpu.VMEM((256, 128), F32), *seps, v_other, v_near, near(skew), near(part))
+    rows = near(lax.all_to_all(rows, AXES, 0, 0, tiled=True))
+    return call(end_kernel, jax.ShapeDtypeStruct((3, 16), F32), rows)
 
 
 def solution(mesh):

time: 56.1 us -> 47.9 us (0.85)
  Pallas kernels: 11.1 us -> 6.88 us
  local copies, waits for them, and re-layouts: 4.81 us -> 1.16 us
  blocking collectives: 27.9 us -> 25.1 us
  waiting for transfers between devices: 0.08 us -> 1.46 us
  starting transfers between devices: 11.9 us -> 13 us
    pallas_call x4 -> x5, Pallas kernels: 11.1 us -> 6.88 us  [call(): pl.pallas_call(kernel, out_shape=out, in_specs=specs, out_specs=VMEM)(*args)]
    unnamed x18 -> x2, local copies, waits for them, and re-layouts: 2.89 us -> 0.01 us
    all_to_all x1, blocking collectives: 27.9 us -> 25.1 us  [local(): rows = near(lax.all_to_all(rows, AXES, 0, 0, tiled=True))]
    ppermute x5, waiting for transfers between devices: 0.08 us -> 1.46 us  [send(): return near(lax.ppermute(value, AXES, pairs))]
    ppermute x5, starting transfers between devices: 11.9 us -> 13 us  [send(): return near(lax.ppermute(value, AXES, pairs))]
    slice x1 -> x0, local copies, waits for them, and re-layouts: 0.69 us -> none  [local(): part[:1]]
where the time goes in v2:
time: 47.9 us; the launch traced here: 47.7 us
  blocking collectives  25.1 us (52%)
  starting transfers between devices  13 us (27%)
  Pallas kernels  6.88 us (14%)
  waiting for transfers between devices  1.46 us (3%)
  local copies, waits for them, and re-layouts  1.16 us (2%)
    all_to_all x1, blocking collectives, local(): rows = near(lax.all_to_all(rows, AXES, 0, 0, tiled=True))  25.1 us
    ppermute x5, starting transfers between devices, send(): return near(lax.ppermute(value, AXES, pairs))  13 us
    pallas_call x5, Pallas kernels, call(): pl.pallas_call(kernel, out_shape=out, in_specs=specs, out_specs=VMEM)(*args)  6.88 us
    ppermute x5, waiting for transfers between devices, send(): return near(lax.ppermute(value, AXES, pairs))  1.46 us
    dynamic_slice x1, local copies, waits for them, and re-layouts, local(): v_keep = lax.dynamic_slice_in_dim(v, 4 * half, 4, 0)  1.12 us
  transfers between devices with their start and end apart: 5, of which 1 were waited for; matrix products, arithmetic and copies ran while one was open for 0% of the time, Pallas kernels for 10%

profile of v2, /device:TPU:1, one launch (start us, length us, event | category | flops | bytes accessed | tf_op | source)
XLA Modules:
  0.0 47.7 jit_solution(9710802690300913753)
XLA Ops:
  0.0 0.0 copy-start
  0.0 1.1 %constant_dynamic-slice_fusion.2 = (f32[4,64,256]{2,1,0:T(8,128)S(1)}, f32[4,64,256]{2,1,0:T(8,128)S(1)}) fusion(f32[8,64,256]{2,1,0:T(8,128)} %v_ref.1, s32[]{:T(128)S(6)} %select_n.13, s32[]{:T(128)S(6)} %select_n.12), kind=kLoop, calls=%fused_computation.2 | loop fusion | bytes 1048584 | tf_op jit(solution)/shard_map/dynamic_slice | solution.py:187
  1.1 3.6 %collective-permute-start = (f32[4,64,256]{2,1,0:T(8,128)S(1)}, f32[4,64,256]{2,1,0:T(8,128)S(1)}, u32[]{:S(2)}, u32[]{:S(2)}) collective-permute-start(f32[4,64,256]{2,1,0:T(8,128)S(1)} %get-tuple-element.8), channel_id=1, source_target_pairs={{0,32},{1,33},{2,34},{3,35},{4,36},{5,37},{6,38},{7,39},{8,40},{9,... | collective-permute-start | bytes 786440 | tf_op jit(solution)/shard_map/ppermute | solution.py:179
  4.8 0.0 copy-done
  4.8 1.0 %collective-permute-start.2 = (f32[4,64,256]{2,1,0:T(8,128)S(1)}, f32[4,64,256]{2,1,0:T(8,128)S(1)}, u32[]{:S(2)}, u32[]{:S(2)}) collective-permute-start(f32[4,64,256]{2,1,0:T(8,128)S(1)} %get-tuple-element.5.send), channel_id=1, source_target_pairs={{0,1},{1,0},{2,3},{3,2},{4,5},{5,4},{6,7},{7,6},{8,9},{9,8},{10,11... | collective-permute-start | bytes 786440 | tf_op jit(solution)/shard_map/ppermute | solution.py:179
  5.9 5.6 %collective-permute-start.4 = (f32[4,64,256]{2,1,0:T(8,128)S(1)}, f32[4,64,256]{2,1,0:T(8,128)S(1)}, u32[]{:S(2)}, u32[]{:S(2)}) collective-permute-start(f32[4,64,256]{2,1,0:T(8,128)S(1)} %get-tuple-element.5.send), channel_id=1, source_target_pairs={{0,2},{1,31},{2,4},{3,1},{4,6},{5,3},{6,8},{7,5},{8,10},{9,7},{10,... | collective-permute-start | bytes 786440 | tf_op jit(solution)/shard_map/ppermute | solution.py:179
  11.5 0.0 collective-permute-start.3
  11.5 2.7 %collective-permute-start.1 = (f32[4,64,256]{2,1,0:T(8,128)S(1)}, f32[4,64,256]{2,1,0:T(8,128)S(1)}, u32[]{:S(2)}, u32[]{:S(2)}) collective-permute-start(f32[4,64,256]{2,1,0:T(8,128)S(1)} %get-tuple-element.7.own), channel_id=1, source_target_pairs={{0,192},{1,193},{2,194},{3,195},{4,196},{5,197},{6,198},{7,199},{8... | collective-permute-start | bytes 786440 | tf_op jit(solution)/shard_map/ppermute | solution.py:179
  14.2 2.6 %shard_map.65.before = f32[8,128]{1,0:T(8,128)S(1)} custom-call(s32[16]{0:T(128)} %sx.5, s32[16]{0:T(128)} %sy.5, s32[16]{0:T(128)} %sz.5, f32[8,64,256]{2,1,0:T(8,128)} %u_ref.1, f32[8,64,256]{2,1,0:T(8,128)} %v_ref.1, f32[8,64,256]{2,1,0:T(8,128)} %w_ref.1), custom_call_target="tpu_custom_call" | custom-call | tf_op jit(solution)/shard_map/pallas_call | solution.py:171
  16.8 0.0 collective-permute-done.other
  16.8 0.5 %shard_map.64.skew = f32[8,512]{1,0:T(8,128)S(1)} custom-call(f32[4,64,256]{2,1,0:T(8,128)S(1)} %get-tuple-element.7.own, f32[4,64,256]{2,1,0:T(8,128)S(1)} %collective-permute-done.other), custom_call_target="tpu_custom_call" | custom-call | tf_op jit(solution)/shard_map/pallas_call | solution.py:171
  17.3 0.0 collective-permute-done.2.other
  17.3 0.0 collective-permute-done.4.near_send
  17.3 1.4 %collective-permute-done.3.near_keep = f32[4,64,256]{2,1,0:T(8,128)S(1)} collective-permute-done((f32[4,64,256]{2,1,0:T(8,128)S(1)}, f32[4,64,256]{2,1,0:T(8,128)S(1)}, u32[]{:S(2)}, u32[]{:S(2)}) %collective-permute-start.3) | collective-permute-done | bytes 262176 | tf_op jit(solution)/shard_map/ppermute | solution.py:179
  18.8 1.7 %shard_map.66.before = f32[8,128]{1,0:T(8,128)S(1)} custom-call(s32[16]{0:T(128)} %sx.5, s32[16]{0:T(128)} %sy.5, s32[16]{0:T(128)} %sz.5, f32[4,64,256]{2,1,0:T(8,128)S(1)} %get-tuple-element.6.keep, f32[4,64,256]{2,1,0:T(8,128)S(1)} %get-tuple-element.5.send, f32[4,64,256]{2,1,0:T(8,128)S(1)} %collective-permute-done.2.other, ...), custom_call_target="tpu_custom_call" | custom-call | tf_op jit(solution)/shard_map/pallas_call | solution.py:171
  20.5 0.0 collective-permute-done.1.near
  20.5 1.3 %shard_map.67 = f32[256,128]{1,0:T(8,128)S(1)} custom-call(s32[16]{0:T(128)} %sx.5, s32[16]{0:T(128)} %sy.5, s32[16]{0:T(128)} %sz.5, f32[4,64,256]{2,1,0:T(8,128)S(1)} %collective-permute-done.other, f32[4,64,256]{2,1,0:T(8,128)S(1)} %collective-permute-done.1.near, f32[8,512]{1,0:T(8,128)S(1)} %shard_map.64.skew, f32[8,128]{1,0:T(8,128)S(1)} %shard_map.66.before), custom_call_target="tpu_custom_call" | custom-call | tf_op jit(solution)/shard_map/pallas_call | solution.py:171
  21.8 25.1 %all_to_all.11 = f32[256,1,128]{2,1,0:T(1,128)S(1)} all-to-all(f32[256,1,128]{2,1,0:T(1,128)S(1)} %bitcast.5), channel_id=1, replica_groups=mesh['y'=4,'xh'=2,'xl'=2,'z'=8,'c'=2] {'y','xh','xl','z','c'}, dimensions={0} | all-to-all | bytes 262144 | tf_op jit(solution)/shard_map/all_to_all | solution.py:200
  46.9 0.8 %shard_map.68 = f32[3,16]{1,0:T(4,128)} custom-call(f32[256,128]{1,0:T(8,128)S(1)} %bitcast.4), custom_call_target="tpu_custom_call" | custom-call | tf_op jit(solution)/shard_map/pallas_call | solution.py:171
  (1 shorter events, 0.0 us)
Async XLA Ops:
  0.0 4.8 %copy-start = (f32[8,64,256]{2,1,0:T(8,128)S(1)}, f32[8,64,256]{2,1,0:T(8,128)}, u32[]{:S(2)}) copy-start(f32[8,64,256]{2,1,0:T(8,128)} %u_ref.1) | copy-start | bytes 1572868
  1.1 15.7 %collective-permute-start = (f32[4,64,256]{2,1,0:T(8,128)S(1)}, f32[4,64,256]{2,1,0:T(8,128)S(1)}, u32[]{:S(2)}, u32[]{:S(2)}) collective-permute-start(f32[4,64,256]{2,1,0:T(8,128)S(1)} %get-tuple-element.8), channel_id=1, source_target_pairs={{0,32},{1,33},{2,34},{3,35},{4,36},{5,37},{6,38},{7,39},{8,40},{9,... | collective-permute-start | bytes 786440 | tf_op jit(solution)/shard_map/ppermute | solution.py:179
  4.8 12.5 %collective-permute-start.2 = (f32[4,64,256]{2,1,0:T(8,128)S(1)}, f32[4,64,256]{2,1,0:T(8,128)S(1)}, u32[]{:S(2)}, u32[]{:S(2)}) collective-permute-start(f32[4,64,256]{2,1,0:T(8,128)S(1)} %get-tuple-element.5.send), channel_id=1, source_target_pairs={{0,1},{1,0},{2,3},{3,2},{4,5},{5,4},{6,7},{7,6},{8,9},{9,8},{10,11... | collective-permute-start | bytes 786440 | tf_op jit(solution)/shard_map/ppermute | solution.py:179
  5.9 11.5 %collective-permute-start.4 = (f32[4,64,256]{2,1,0:T(8,128)S(1)}, f32[4,64,256]{2,1,0:T(8,128)S(1)}, u32[]{:S(2)}, u32[]{:S(2)}) collective-permute-start(f32[4,64,256]{2,1,0:T(8,128)S(1)} %get-tuple-element.5.send), channel_id=1, source_target_pairs={{0,2},{1,31},{2,4},{3,1},{4,6},{5,3},{6,8},{7,5},{8,10},{9,7},{10,... | collective-permute-start | bytes 786440 | tf_op jit(solution)/shard_map/ppermute | solution.py:179
  11.5 7.3 %collective-permute-start.3 = (f32[4,64,256]{2,1,0:T(8,128)S(1)}, f32[4,64,256]{2,1,0:T(8,128)S(1)}, u32[]{:S(2)}, u32[]{:S(2)}) collective-permute-start(f32[4,64,256]{2,1,0:T(8,128)S(1)} %get-tuple-element.6.keep), channel_id=1, source_target_pairs={{0,30},{1,3},{2,0},{3,5},{4,2},{5,7},{6,4},{7,9},{8,6},{9,11},{10,... | collective-permute-start | bytes 786440 | tf_op jit(solution)/shard_map/ppermute | solution.py:179
  11.5 9.1 %collective-permute-start.1 = (f32[4,64,256]{2,1,0:T(8,128)S(1)}, f32[4,64,256]{2,1,0:T(8,128)S(1)}, u32[]{:S(2)}, u32[]{:S(2)}) collective-permute-start(f32[4,64,256]{2,1,0:T(8,128)S(1)} %get-tuple-element.7.own), channel_id=1, source_target_pairs={{0,192},{1,193},{2,194},{3,195},{4,196},{5,197},{6,198},{7,199},{8... | collective-permute-start | bytes 786440 | tf_op jit(solution)/shard_map/ppermute | solution.py:179

commit v3 on v2

--- a/solution.py
+++ b/solution.py
@@ -15,7 +15,7 @@
 HIGH = lax.Precision.HIGHEST
 
 
-def pairs_of(target):
+def pairs_of(target, sends=lambda *at: True):
     def flat(at):
         index = 0
         for size, i in zip(SHAPE, at):
@@ -25,22 +25,18 @@
     places = [()]
     for size in SHAPE:
         places = [at + (i,) for at in places for i in range(size)]
-    return [(flat(at), flat(target(*at))) for at in places]
+    return [(flat(at), flat(target(*at))) for at in places if sends(*at)]
 
 
-def u_target(step):
-    def target(y, xh, xl, z, c):
-        chip = (xl * 8 + z + step(c)) % 16
-        return (y, xh, chip // 8, chip % 8, c)
-
-    return target
+def chip_step(y, xh, xl, z, c):
+    chip = xl * 8 + z + (1 if c else -1)
+    return (y, xh, chip // 8, chip % 8, c)
 
 
-U_KEEP = pairs_of(u_target(lambda c: -1 if c == 0 else 1))
-U_SEND = pairs_of(u_target(lambda c: 1 if c == 0 else -1))
-CORES = pairs_of(lambda y, xh, xl, z, c: (y, xh, xl, z, 1 - c))
-V_SWAP = pairs_of(lambda y, xh, xl, z, c: (y, 1 - xh, xl, z, c))
-V_KEEP = pairs_of(lambda y, xh, xl, z, c: (y - 1 if xh == 0 else y + 1, xh, xl, z, c))
+U_CHIP = pairs_of(chip_step)
+U_CORE = pairs_of(lambda y, xh, xl, z, c: (y, xh, xl, z, 1 - c))
+V_HALF = pairs_of(lambda y, xh, xl, z, c: (y, c, xl, z, c), lambda y, xh, xl, z, c: xh != c)
+V_NEXT = pairs_of(lambda y, xh, xl, z, c: (y + (1 if xh else -1), xh, xl, z, c), lambda y, xh, xl, z, c: xh == c)
 
 
 def dot_nt(a, b):
@@ -116,42 +112,38 @@
     out_ref[...] = jnp.where(of_u, u_sums, jnp.where(of_v, v_sums, w_sums))
 
 
-def swap_kernel(own, other, out_ref):
-    gram = dot_tn(own[...].reshape(256, 256), other[...].reshape(256, 256))
-    out_ref[...] = skewed(widened(gram))
+def v_kernel(sx, sy, sz, own, other, near, before, out_ref):
+    half = lax.axis_index("xh")
+    works = half == lax.axis_index("c")
+
+    @pl.when(works)
+    def _():
+        lags = lag_row((sx, sy, sz))
+        lane = lane_index()
+        middle = other[...].reshape(512, 256)
+        gram = dot_tn(own[...].reshape(512, 256), middle) + dot_tn(middle, near[...].reshape(512, 256))
+        sums = pick(skewed(widened(gram)), jnp.where(half == 0, lags - 256, 256 - lags))
+        out_ref[...] = before[...] + jnp.where((lane >= 16) & (lane < 32), sums, 0.0)
+
+    @pl.when(jnp.logical_not(works))
+    def _():
+        out_ref[...] = before[...]
 
 
-def last_kernel(sx, sy, sz, other, near, skew, before, out_ref):
+def u_kernel(sx, sy, sz, own, other, near, before, out_ref):
     lags = lag_row((sx, sy, sz))
-    lane = lane_index()
-    first = lax.axis_index("xh") == 0
-    gram = dot_tn(other[...].reshape(256, 256), near[...].reshape(256, 256))
-    total = skew[...] + skewed(widened(gram))
-    sums = pick(total, jnp.where(first, lags - 256, 256 - lags))
-    row = before[...] + jnp.where((lane >= 16) & (lane < 32), sums, 0.0)
+    first = lax.axis_index("c") == 0
+    grams = jnp.zeros((128, 64), F32)
+    for z in range(8):
+        early = jnp.where(first, own[z], near[z])
+        late = jnp.where(first, near[z], own[z])
+        grams = grams + dot_nt(jnp.concatenate([other[z], early], axis=0), late)
+    i = lax.broadcasted_iota(jnp.int32, (64, 64), 0)
+    j = lax.broadcasted_iota(jnp.int32, (64, 64), 1)
+    gram = jnp.concatenate([grams[:64], jnp.where(j <= i, grams[64:], 0.0)], axis=1)
+    row = before[...] + jnp.where(lane_index() < 16, pick(skewed(gram), lags - 64), 0.0)
     for i in range(0, out_ref.shape[0], 8):
         out_ref[i : i + 8] = row
-
-
-def u_kernel(sx, sy, sz, keep, send, other, near_keep, near_send, before, out_ref):
-    lags = lag_row((sx, sy, sz))
-    lane = lane_index()
-    first = lax.axis_index("c") == 0
-    left = jnp.zeros((64, 128), F32)
-    right = jnp.zeros((64, 64), F32)
-    pad = jnp.zeros((64, 64), F32)
-    for z in range(4):
-        a, b, c = keep[z], other[z], near_keep[z]
-        both = dot_nt(jnp.concatenate([a, b], axis=0), jnp.concatenate([b, c], axis=0))
-        left = left + both[:64] + jnp.concatenate([both[64:, 64:], pad], axis=1)
-        right = right + dot_nt(near_send[z], send[z])
-    gram = left + jnp.concatenate([pad, right], axis=1)
-    i = lax.broadcasted_iota(jnp.int32, (64, 128), 0)
-    j = lax.broadcasted_iota(jnp.int32, (64, 128), 1) - 64
-    ahead = jnp.where(first, i - j, j - i)
-    gram = jnp.where((j < 0) | (ahead >= 0), gram, 0.0)
-    sums = pick(skewed(gram), jnp.where(first, lags - 64, 64 - lags))
-    out_ref[...] = before[...] + jnp.where(lane < 16, sums, 0.0)
 
 
 def end_kernel(parts, out_ref):
@@ -180,23 +172,15 @@
 
 
 def local(u, v, w, sep_x, sep_y, sep_z):
-    core = lax.axis_index("c")
-    half = lax.axis_index("xh")
-    u_keep = lax.dynamic_slice_in_dim(u, 4 * core, 4, 0)
-    u_send = lax.dynamic_slice_in_dim(u, 4 - 4 * core, 4, 0)
-    v_keep = lax.dynamic_slice_in_dim(v, 4 * half, 4, 0)
-    v_send = lax.dynamic_slice_in_dim(v, 4 - 4 * half, 4, 0)
-    v_other = send(v_send, V_SWAP)
-    u_other = send(u_send, CORES)
-    near_keep = send(u_keep, U_KEEP)
-    near_send = send(u_send, U_SEND)
-    v_near = send(v_keep, V_KEEP)
+    v_other = send(v, V_HALF)
+    v_near = send(v, V_NEXT)
+    u_other = send(u, U_CORE)
+    u_near = send(u, U_CHIP)
     seps = (sep_x, sep_y, sep_z)
     row = pltpu.VMEM((8, 128), F32)
     part = call(own_kernel, row, *seps, u, v, w)
-    skew = call(swap_kernel, pltpu.VMEM((8, 512), F32), near(v_keep), v_other)
-    part = call(u_kernel, row, *seps, near(u_keep), near(u_send), u_other, near_keep, near_send, near(part))
-    rows = call(last_kernel, pltpu.VMEM((256, 128), F32), *seps, v_other, v_near, near(skew), near(part))
+    part = call(v_kernel, row, *seps, v, v_other, v_near, near(part))
+    rows = call(u_kernel, pltpu.VMEM((256, 128), F32), *seps, u, u_other, u_near, near(part))
     rows = near(lax.all_to_all(rows, AXES, 0, 0, tiled=True))
     return call(end_kernel, jax.ShapeDtypeStruct((3, 16), F32), rows)
 

time: 47.9 us -> 49.6 us (1.035)
  waiting for transfers between devices: 1.46 us -> 8.04 us
  starting transfers between devices: 13 us -> 9.42 us
  local copies, waits for them, and re-layouts: 1.16 us -> 0 us
    ppermute x5 -> x4, waiting for transfers between devices: 1.46 us -> 8.04 us  [send(): return near(lax.ppermute(value, AXES, pairs))]
    ppermute x5 -> x4, starting transfers between devices: 13 us -> 9.42 us  [send(): return near(lax.ppermute(value, AXES, pairs))]
    dynamic_slice x2 -> x0, local copies, waits for them, and re-layouts: 1.16 us -> none  [the longest x1 1.12 us: local(): v_keep = lax.dynamic_slice_in_dim(v, 4 * half, 4, 0)]
    pallas_call x5 -> x4, Pallas kernels: 6.88 us -> 6.76 us  [call(): pl.pallas_call(kernel, out_shape=out, in_specs=specs, out_specs=VMEM)(*args)]
  transfers between devices with their start and end apart: 5 -> 4, of which waited for: 1 -> 1; matrix products, arithmetic and copies ran while one was open for 0% -> 0% of each run, Pallas kernels for 10% -> 7%
where the time goes in v3:
time: 49.6 us; the launch traced here: 49.4 us
  blocking collectives  25.1 us (51%)
  starting transfers between devices  9.42 us (19%)
  waiting for transfers between devices  8.04 us (16%)
  Pallas kernels  6.76 us (14%)
    all_to_all x1, blocking collectives, local(): rows = near(lax.all_to_all(rows, AXES, 0, 0, tiled=True))  25.1 us
    ppermute x4, starting transfers between devices, send(): return near(lax.ppermute(value, AXES, pairs))  9.42 us
    ppermute x4, waiting for transfers between devices, send(): return near(lax.ppermute(value, AXES, pairs))  8.04 us
    pallas_call x4, Pallas kernels, call(): pl.pallas_call(kernel, out_shape=out, in_specs=specs, out_specs=VMEM)(*args)  6.76 us
  transfers between devices with their start and end apart: 4, of which 1 were waited for; matrix products, arithmetic and copies ran while one was open for 0% of the time, Pallas kernels for 7%

profile of v3, /device:TPU:1, one launch (start us, length us, event | category | flops | bytes accessed | tf_op | source)
XLA Modules:
  0.0 49.4 jit_solution(4540198006299461255)
XLA Ops:
  0.0 5.5 %collective-permute-start.2 = (f32[8,64,256]{2,1,0:T(8,128)}, f32[8,64,256]{2,1,0:T(8,128)S(1)}, u32[]{:S(2)}, u32[]{:S(2)}) collective-permute-start(f32[8,64,256]{2,1,0:T(8,128)} %own.2), channel_id=1, source_target_pairs={{1,33},{3,35},{5,37},{7,39},{9,41},{11,43},{13,45},{15,47},{17,49}... | collective-permute-start | bytes 1572872 | tf_op jit(solution)/shard_map/ppermute | solution.py:171
  5.5 0.7 %collective-permute-start.3 = (f32[8,64,256]{2,1,0:T(8,128)}, f32[8,64,256]{2,1,0:T(8,128)S(1)}, u32[]{:S(2)}, u32[]{:S(2)}) collective-permute-start(f32[8,64,256]{2,1,0:T(8,128)} %own.2), channel_id=1, source_target_pairs={{0,192},{2,194},{4,196},{6,198},{8,200},{10,202},{12,204},{14,206}... | collective-permute-start | bytes 1572872 | tf_op jit(solution)/shard_map/ppermute | solution.py:171
  6.2 1.6 %collective-permute-start = (f32[8,64,256]{2,1,0:T(8,128)}, f32[8,64,256]{2,1,0:T(8,128)S(1)}, u32[]{:S(2)}, u32[]{:S(2)}) collective-permute-start(f32[8,64,256]{2,1,0:T(8,128)} %own.3), channel_id=1, source_target_pairs={{0,1},{1,0},{2,3},{3,2},{4,5},{5,4},{6,7},{7,6},{8,9},{9,8},{10,11... | collective-permute-start | bytes 1572872 | tf_op jit(solution)/shard_map/ppermute | solution.py:171
  7.8 1.6 %collective-permute-start.1 = (f32[8,64,256]{2,1,0:T(8,128)}, f32[8,64,256]{2,1,0:T(8,128)S(1)}, u32[]{:S(2)}, u32[]{:S(2)}) collective-permute-start(f32[8,64,256]{2,1,0:T(8,128)} %own.3), channel_id=1, source_target_pairs={{0,30},{1,3},{2,0},{3,5},{4,2},{5,7},{6,4},{7,9},{8,6},{9,11},{10,... | collective-permute-start | bytes 1572872 | tf_op jit(solution)/shard_map/ppermute | solution.py:171
  9.4 2.6 %shard_map.64.before = f32[8,128]{1,0:T(8,128)S(1)} custom-call(s32[16]{0:T(128)} %sx.5, s32[16]{0:T(128)} %sy.5, s32[16]{0:T(128)} %sz.5, f32[8,64,256]{2,1,0:T(8,128)} %own.3, f32[8,64,256]{2,1,0:T(8,128)} %own.2, f32[8,64,256]{2,1,0:T(8,128)} %w_ref.1), custom_call_target="tpu_custom_call" | custom-call | tf_op jit(solution)/shard_map/pallas_call | solution.py:163
  12.1 0.0 collective-permute-done.2.other
  12.1 0.0 collective-permute-done.3.near
  12.1 1.1 %shard_map.65.before = f32[8,128]{1,0:T(8,128)S(1)} custom-call(s32[16]{0:T(128)} %sx.5, s32[16]{0:T(128)} %sy.5, s32[16]{0:T(128)} %sz.5, f32[8,64,256]{2,1,0:T(8,128)} %own.2, f32[8,64,256]{2,1,0:T(8,128)S(1)} %collective-permute-done.2.other, f32[8,64,256]{2,1,0:T(8,128)S(1)} %collective-permute-done.3.near, f32[8,128]{1,0:T(8,128)S(1)} %shard_map.64.before), custom_call_target="tpu_custom_call" | custom-call | tf_op jit(solution)/shard_map/pallas_call | solution.py:163
  13.2 0.0 collective-permute-done.other
  13.2 8.0 %collective-permute-done.1.near = f32[8,64,256]{2,1,0:T(8,128)S(1)} collective-permute-done((f32[8,64,256]{2,1,0:T(8,128)}, f32[8,64,256]{2,1,0:T(8,128)S(1)}, u32[]{:S(2)}, u32[]{:S(2)}) %collective-permute-start.1) | collective-permute-done | bytes 524320 | tf_op jit(solution)/shard_map/ppermute | solution.py:171
  21.2 2.3 %shard_map.66 = f32[256,128]{1,0:T(8,128)S(1)} custom-call(s32[16]{0:T(128)} %sx.5, s32[16]{0:T(128)} %sy.5, s32[16]{0:T(128)} %sz.5, f32[8,64,256]{2,1,0:T(8,128)} %own.3, f32[8,64,256]{2,1,0:T(8,128)S(1)} %collective-permute-done.other, f32[8,64,256]{2,1,0:T(8,128)S(1)} %collective-permute-done.1.near, f32[8,128]{1,0:T(8,128)S(1)} %shard_map.65.before), custom_call_target="tpu_custom_call" | custom-call | tf_op jit(solution)/shard_map/pallas_call | solution.py:163
  23.5 25.1 %all_to_all.11 = f32[256,1,128]{2,1,0:T(1,128)S(1)} all-to-all(f32[256,1,128]{2,1,0:T(1,128)S(1)} %bitcast.5), channel_id=1, replica_groups=mesh['y'=4,'xh'=2,'xl'=2,'z'=8,'c'=2] {'y','xh','xl','z','c'}, dimensions={0} | all-to-all | bytes 262144 | tf_op jit(solution)/shard_map/all_to_all | solution.py:184
  48.6 0.8 %shard_map.67 = f32[3,16]{1,0:T(4,128)} custom-call(f32[256,128]{1,0:T(8,128)S(1)} %bitcast.4), custom_call_target="tpu_custom_call" | custom-call | tf_op jit(solution)/shard_map/pallas_call | solution.py:163
Async XLA Ops:
  0.0 12.1 %collective-permute-start.2 = (f32[8,64,256]{2,1,0:T(8,128)}, f32[8,64,256]{2,1,0:T(8,128)S(1)}, u32[]{:S(2)}, u32[]{:S(2)}) collective-permute-start(f32[8,64,256]{2,1,0:T(8,128)} %own.2), channel_id=1, source_target_pairs={{1,33},{3,35},{5,37},{7,39},{9,41},{11,43},{13,45},{15,47},{17,49}... | collective-permute-start | bytes 1572872 | tf_op jit(solution)/shard_map/ppermute | solution.py:171
  5.5 6.6 %collective-permute-start.3 = (f32[8,64,256]{2,1,0:T(8,128)}, f32[8,64,256]{2,1,0:T(8,128)S(1)}, u32[]{:S(2)}, u32[]{:S(2)}) collective-permute-start(f32[8,64,256]{2,1,0:T(8,128)} %own.2), channel_id=1, source_target_pairs={{0,192},{2,194},{4,196},{6,198},{8,200},{10,202},{12,204},{14,206}... | collective-permute-start | bytes 1572872 | tf_op jit(solution)/shard_map/ppermute | solution.py:171
  6.2 7.0 %collective-permute-start = (f32[8,64,256]{2,1,0:T(8,128)}, f32[8,64,256]{2,1,0:T(8,128)S(1)}, u32[]{:S(2)}, u32[]{:S(2)}) collective-permute-start(f32[8,64,256]{2,1,0:T(8,128)} %own.3), channel_id=1, source_target_pairs={{0,1},{1,0},{2,3},{3,2},{4,5},{5,4},{6,7},{7,6},{8,9},{9,8},{10,11... | collective-permute-start | bytes 1572872 | tf_op jit(solution)/shard_map/ppermute | solution.py:171
  7.8 13.4 %collective-permute-start.1 = (f32[8,64,256]{2,1,0:T(8,128)}, f32[8,64,256]{2,1,0:T(8,128)S(1)}, u32[]{:S(2)}, u32[]{:S(2)}) collective-permute-start(f32[8,64,256]{2,1,0:T(8,128)} %own.3), channel_id=1, source_target_pairs={{0,30},{1,3},{2,0},{3,5},{4,2},{5,7},{6,4},{7,9},{8,6},{9,11},{10,... | collective-permute-start | bytes 1572872 | tf_op jit(solution)/shard_map/ppermute | solution.py:171

commit v4 on v2

v4 whole, which is shorter than its diff:
```python
import jax
import jax.numpy as jnp
from jax import lax
from jax.experimental import pallas as pl
from jax.experimental.pallas import tpu as pltpu
from jax.sharding import Mesh
from jax.sharding import PartitionSpec as P


SHAPE = (4, 2, 2, 8, 2)
AXES = ("y", "xh", "xl", "z", "c")
SERVED = AXES
GX = ("xl", "z", "c")
GY = ("y", "xh")
F32 = jnp.float32
BF16 = jnp.bfloat16
HIGH = lax.Precision.HIGHEST


def pairs_of(target):
    def flat(at):
        index = 0
        for size, i in zip(SHAPE, at):
            index = index * size + i % size
        return index

    places = [()]
    for size in SHAPE:
        places = [at + (i,) for at in places for i in range(size)]
    return [(flat(at), flat(target(*at))) for at in places]


def chip_step(step):
    def target(y, xh, xl, z, c):
        chip = xl * 8 + z + step[c]
        return (y, xh, chip // 8, chip % 8, c)

    return target


U_DOWN = pairs_of(chip_step((-1, -1)))
U_BOTH = pairs_of(chip_step((-1, 1)))
U_CORE = pairs_of(lambda y, xh, xl, z, c: (y, xh, xl, z, 1 - c))
V_SWAP = pairs_of(lambda y, xh, xl, z, c: (y, 1 - xh, xl, z, c))
V_NEXT = pairs_of(lambda y, xh, xl, z, c: (y + (1 if xh else -1), xh, xl, z, c))


def dot_nt(a, b, precision=HIGH):
    return lax.dot_general(a, b, (((1,), (1,)), ((), ())), precision=precision, preferred_element_type=F32)


def dot_tn(a, b):
    return lax.dot_general(a, b, (((0,), (0,)), ((), ())), precision=HIGH, preferred_element_type=F32)


def dot_nn(a, b):
    return lax.dot_general(a, b, (((1,), (0,)), ((), ())), preferred_element_type=F32)


def lane_index():
    return lax.broadcasted_iota(jnp.int32, (8, 128), 1)


def row_index():
    return lax.broadcasted_iota(jnp.int32, (8, 128), 0)


def lag_row(refs):
    lane = lane_index()
    lags = jnp.zeros((8, 128), jnp.int32)
    for axis, ref in enumerate(refs):
        for k in range(16):
            lags = jnp.where(lane == axis * 16 + k, ref[k], lags)
    return lags


def skewed(gram):
    rows, lanes = gram.shape
    total = gram[:8]
    for i in range(8, rows, 8):
        total = total + pltpu.roll(gram[i : i + 8], (lanes - i) % lanes, 1)
    return total


def pick(skew, diagonal):
    lanes = skew.shape[1]
    at = (diagonal + row_index()) & (lanes - 1)
    got = jnp.zeros((8, 128), F32)
    for t in range(lanes // 128):
        part = jnp.take_along_axis(skew[:, t * 128 : (t + 1) * 128], at & 127, axis=1)
        got = jnp.where((at >> 7) == t, part, got)
    return jnp.broadcast_to(jnp.sum(got, axis=0, keepdims=True), (8, 128))


def widened(gram):
    return jnp.concatenate([gram, jnp.zeros(gram.shape, F32)], axis=1)


def halves(x):
    high = x.astype(BF16)
    return high, (x - high.astype(F32)).astype(BF16)


def own_kernel(sx, sy, sz, u_ref, other, v_ref, w_ref, out_ref, u_parts, v_parts):
    lags = lag_row((sx, sy, sz))
    lane = lane_index()
    half = lax.axis_index("xh")
    grams = jnp.zeros((64, 128), F32)
    for z in range(8):
        a, b = u_ref[z], other[z]
        grams = grams + dot_nt(a, jnp.concatenate([a, b], axis=0))
        a_high, a_low = halves(a)
        b_high, b_low = halves(b)
        u_parts[z] = jnp.concatenate([b_high, a_high, b_low, a_low], axis=0)
    u_sums = jnp.where(lags < 64, pick(skewed(widened(grams[:, :64])), lags), 0.0)
    cores = pick(skewed(widened(grams[:, 64:])), 64 - lags)
    counted = (lax.axis_index("c") == 1) & (lags > 0) & (lags < 128)
    u_sums = u_sums + jnp.where(counted, cores, 0.0)
    keep = v_ref[pl.ds(4 * half, 4)].reshape(256, 256).T
    v_parts[:256], v_parts[256:] = halves(keep)
    v_rows = v_ref[...].reshape(512, 256)
    v_sums = pick(skewed(widened(dot_tn(v_rows, v_rows))), lags)
    planes = [w_ref[z] for z in range(8)]
    w_sums = jnp.zeros((8, 128), F32)
    for lag in range(5):
        total = planes[0] * planes[lag]
        for z in range(1, 8 - lag):
            total = total + planes[z] * planes[z + lag]
        total = jnp.sum(jnp.sum(total, axis=0, keepdims=True), axis=1, keepdims=True)
        w_sums = jnp.where(lags == lag, total, w_sums)
    w_sums = w_sums * 8.0 / (8.0 - lags.astype(F32))
    of_u = (lane < 16) | (lane == 48)
    of_v = (lane < 32) | (lane == 49)
    out_ref[...] = jnp.where(of_u, u_sums, jnp.where(of_v, v_sums, w_sums))


def u_kernel(sx, sy, sz, parts, near_down, near_both, before, out_ref):
    lags = lag_row((sx, sy, sz))
    first = lax.axis_index("c") == 0
    sums = []
    for near in (near_down, near_both):
        total = jnp.zeros((128, 64), F32)
        for i in range(4):
            z = i if near is near_down else 4 + i
            high, low = halves(near[i])
            both = dot_nt(parts[z], high, None)
            total = total + both[:128] + both[128:] + dot_nt(parts[z, :128], low, None)
        sums.append(total)
    down, mixed = sums
    far = down[64:] + jnp.where(first, mixed[64:], mixed[64:].T)
    next_to = jnp.where(first, down[:64] + mixed[:64], 0.0)
    i = lax.broadcasted_iota(jnp.int32, (64, 64), 0)
    j = lax.broadcasted_iota(jnp.int32, (64, 64), 1)
    gram = jnp.concatenate([next_to, jnp.where(j <= i, far, 0.0)], axis=1)
    out_ref[...] = before[...] + jnp.where(lane_index() < 16, pick(skewed(gram), lags - 64), 0.0)


def v_kernel(sx, sy, sz, parts, other, near, before, out_ref):
    lags = lag_row((sx, sy, sz))
    lane = lane_index()
    first = lax.axis_index("xh") == 0
    high, low = halves(other[...].reshape(256, 256))
    near_high, near_low = halves(near[...].reshape(256, 256).T)
    i = lax.broadcasted_iota(jnp.int32, (256, 256), 0)
    j = lax.broadcasted_iota(jnp.int32, (256, 256), 1)
    ahead = jnp.where(first, i - j, j - i)
    sums = jnp.zeros((8, 128), F32)
    for a_high, a_low, sign in ((parts[:256], parts[256:], 1), (near_high, near_low, -1)):
        gram = dot_nn(a_high, high) + dot_nn(a_low, high) + dot_nn(a_high, low)
        gram = jnp.where(ahead * sign >= 0, gram, 0.0)
        sums = sums + pick(skewed(gram), jnp.where(first, lags - 256, 256 - lags) * sign)
    row = before[...] + jnp.where((lane >= 16) & (lane < 32), sums, 0.0)
    for i in range(0, out_ref.shape[0], 8):
        out_ref[i : i + 8] = row


def end_kernel(parts, out_ref):
    total = jnp.sum(parts[...], axis=0, keepdims=True)
    lane = lax.broadcasted_iota(jnp.int32, (1, 128), 1)
    for axis in range(3):
        energy = jnp.sum(jnp.where(lane == 48 + axis, total, 0.0), axis=1, keepdims=True)
        out_ref[axis : axis + 1, :] = total[:, axis * 16 : axis * 16 + 16] / energy


SMEM = pl.BlockSpec(memory_space=pltpu.SMEM)
VMEM = pl.BlockSpec(memory_space=pltpu.VMEM)


def call(kernel, out, *args):
    specs = [SMEM if a.dtype == jnp.int32 else VMEM for a in args]
    return pl.pallas_call(kernel, out_shape=out, in_specs=specs, out_specs=jax.tree.map(lambda _: VMEM, out))(*args)


def near(x):
    return pltpu.with_memory_space_constraint(x, pltpu.VMEM)


def send(value, pairs):
    return near(lax.ppermute(value, AXES, pairs))


def local(u, v, w, sep_x, sep_y, sep_z):
    half = lax.axis_index("xh")
    v_keep = lax.dynamic_slice_in_dim(v, 4 * half, 4, 0)
    v_send = lax.dynamic_slice_in_dim(v, 4 - 4 * half, 4, 0)
    v_other = send(v_send, V_SWAP)
    down = send(u[:4], U_DOWN)
    both = send(u[4:], U_BOTH)
    u_other = send(u, U_CORE)
    v_near = send(v_keep, V_NEXT)
    seps = (sep_x, sep_y, sep_z)
    row = pltpu.VMEM((8, 128), F32)
    outs = (row, pltpu.VMEM((8, 256, 256), BF16), pltpu.VMEM((512, 256), BF16))
    part, u_parts, v_parts = call(own_kernel, outs, *seps, u, u_other, v, w)
    part = call(u_kernel, row, *seps, near(u_parts), down, both, near(part))
    rows = call(v_kernel, pltpu.VMEM((256, 128), F32), *seps, near(v_parts), v_other, v_near, near(part))
    rows = near(lax.all_to_all(rows, SERVED, 0, 0, tiled=True))
    return call(end_kernel, jax.ShapeDtypeStruct((3, 16), F32), rows)


def solution(mesh):
    finer = Mesh(mesh.devices.reshape(SHAPE), AXES)
    placed = (P(None, GX, GY),) * 3 + (P(),) * 3
    return jax.shard_map(local, mesh=finer, in_specs=placed, out_specs=P(), check_vma=False)
```

time: 47.9 us -> 50.4 us (1.052)
  local copies, waits for them, and re-layouts: 1.16 us -> 2.6 us
  blocking collectives: 25.1 us -> 26.3 us
    slice x0 -> x1, local copies, waits for them, and re-layouts: none -> 1.87 us  [local(): both = send(u[4:], U_BOTH)]
    all_to_all x1, blocking collectives: 25.1 us -> 26.3 us  [local(): rows = near(lax.all_to_all(rows, SERVED, 0, 0, tiled=True))]
    pallas_call x5 -> x4, Pallas kernels: 6.88 us -> 6.87 us  [call(): pl.pallas_call(kernel, out_shape=out, in_specs=specs, out_specs=jax.tree....]
  transfers between devices with their start and end apart: 5 -> 5, of which waited for: 1 -> 1; matrix products, arithmetic and copies ran while one was open for 0% -> 5% of each run, Pallas kernels for 10% -> 10%
where the time goes in v4:
time: 50.4 us; the launch traced here: 50.3 us
  blocking collectives  26.3 us (52%)
  starting transfers between devices  13.2 us (26%)
  Pallas kernels  6.87 us (14%)
  local copies, waits for them, and re-layouts  2.6 us (5%)
  waiting for transfers between devices  1.32 us (3%)
    all_to_all x1, blocking collectives, local(): rows = near(lax.all_to_all(rows, SERVED, 0, 0, tiled=True))  26.3 us
    ppermute x5, starting transfers between devices, send(): return near(lax.ppermute(value, AXES, pairs))  13.2 us
    pallas_call x4, Pallas kernels, call(): pl.pallas_call(kernel, out_shape=out, in_specs=specs, out_specs=jax.tree....  6.87 us
    slice x1, local copies, waits for them, and re-layouts, local(): both = send(u[4:], U_BOTH)  1.87 us
    ppermute x5, waiting for transfers between devices, send(): return near(lax.ppermute(value, AXES, pairs))  1.32 us
  transfers between devices with their start and end apart: 5, of which 1 were waited for; matrix products, arithmetic and copies ran while one was open for 5% of the time, Pallas kernels for 10%

profile of v4, /device:TPU:1, one launch (start us, length us, event | category | flops | bytes accessed | tf_op | source)
XLA Modules:
  0.0 50.3 jit_solution(10455337587472333476)
XLA Ops:
  0.0 0.0 copy-start
  0.0 3.2 %collective-permute-start = (f32[8,64,256]{2,1,0:T(8,128)}, f32[8,64,256]{2,1,0:T(8,128)S(1)}, u32[]{:S(2)}, u32[]{:S(2)}) collective-permute-start(f32[8,64,256]{2,1,0:T(8,128)} %u_ref.1), channel_id=1, source_target_pairs={{0,1},{1,0},{2,3},{3,2},{4,5},{5,4},{6,7},{7,6},{8,9},{9,8},{10,11... | collective-permute-start | bytes 1572872 | tf_op jit(solution)/shard_map/ppermute | solution.py:199
  3.2 1.9 %fusion = (f32[4,64,256]{2,1,0:T(8,128)}, f32[4,64,256]{2,1,0:T(8,128)}) fusion(f32[8,64,256]{2,1,0:T(8,128)} %u_ref.1), kind=kLoop, calls=%fused_computation.2 | loop fusion | bytes 1048576 | tf_op jit(solution)/shard_map/slice | solution.py:208
  5.1 4.8 %collective-permute-start.3 = (f32[4,64,256]{2,1,0:T(8,128)}, f32[4,64,256]{2,1,0:T(8,128)S(1)}, u32[]{:S(2)}, u32[]{:S(2)}) collective-permute-start(f32[4,64,256]{2,1,0:T(8,128)} %get-tuple-element.12), channel_id=1, source_target_pairs={{0,30},{1,31},{2,0},{3,1},{4,2},{5,3},{6,4},{7,5},{8,6},{9,7},{10,... | collective-permute-start | bytes 786440 | tf_op jit(solution)/shard_map/ppermute | solution.py:199
  9.9 0.0 collective-permute-start.4
  9.9 0.0 copy-done
  9.9 0.7 %constant_dynamic-slice_fusion = (f32[4,64,256]{2,1,0:T(8,128)S(1)}, f32[4,64,256]{2,1,0:T(8,128)}) fusion(f32[8,64,256]{2,1,0:T(8,128)S(1)} %copy-done, s32[]{:T(128)S(6)} %select_n.7, s32[]{:T(128)S(6)} %select_n.6), kind=kLoop, calls=%fused_computation | loop fusion | bytes 1048584 | tf_op jit(solution)/shard_map/dynamic_slice | solution.py:204
  10.6 2.5 %collective-permute-start.1 = (f32[4,64,256]{2,1,0:T(8,128)}, f32[4,64,256]{2,1,0:T(8,128)S(1)}, u32[]{:S(2)}, u32[]{:S(2)}) collective-permute-start(f32[4,64,256]{2,1,0:T(8,128)} %get-tuple-element.14), channel_id=1, source_target_pairs={{0,32},{1,33},{2,34},{3,35},{4,36},{5,37},{6,38},{7,39},{8,40},{9,... | collective-permute-start | bytes 786440 | tf_op jit(solution)/shard_map/ppermute | solution.py:199
  13.1 2.7 %collective-permute-start.2 = (f32[4,64,256]{2,1,0:T(8,128)S(1)}, f32[4,64,256]{2,1,0:T(8,128)S(1)}, u32[]{:S(2)}, u32[]{:S(2)}) collective-permute-start(f32[4,64,256]{2,1,0:T(8,128)S(1)} %get-tuple-element.13), channel_id=1, source_target_pairs={{0,192},{1,193},{2,194},{3,195},{4,196},{5,197},{6,198},{7,199},{8... | collective-permute-start | bytes 786440 | tf_op jit(solution)/shard_map/ppermute | solution.py:199
  15.8 0.0 collective-permute-done.other
  15.8 3.3 %shard_map.64 = (f32[8,128]{1,0:T(8,128)S(1)}, bf16[8,256,256]{2,1,0:T(8,128)(2,1)S(1)}, bf16[512,256]{1,0:T(8,128)(2,1)S(1)}) custom-call(s32[16]{0:T(128)} %sx.5, s32[16]{0:T(128)} %sy.5, s32[16]{0:T(128)} %sz.5, f32[8,64,256]{2,1,0:T(8,128)} %u_ref.1, f32[8,64,256]{2,1,0:T(8,128)S(1)} %collective-permute-done.other, f32[8,64,256]{2,1,0:T(8,128)} %v_ref.1, ...), custom_call_target="tpu_custom_call" | custom-call | tf_op jit(solution)/shard_map/pallas_call | solution.py:191
  19.1 0.0 collective-permute-done.3.near_down
  19.1 0.0 collective-permute-done.4.near_both
  19.1 1.5 %shard_map.65.before = f32[8,128]{1,0:T(8,128)S(1)} custom-call(s32[16]{0:T(128)} %sx.5, s32[16]{0:T(128)} %sy.5, s32[16]{0:T(128)} %sz.5, bf16[8,256,256]{2,1,0:T(8,128)(2,1)S(1)} %get-tuple-element.9.parts, f32[4,64,256]{2,1,0:T(8,128)S(1)} %collective-permute-done.3.near_down, f32[4,64,256]{2,1,0:T(8,128)S(1)} %collective-permute-done.4.near_both, ...), custom_call_target="tpu_custom_call" | custom-call | tf_op jit(solution)/shard_map/pallas_call | solution.py:191
  20.7 1.3 %collective-permute-done.1.other = f32[4,64,256]{2,1,0:T(8,128)S(1)} collective-permute-done((f32[4,64,256]{2,1,0:T(8,128)}, f32[4,64,256]{2,1,0:T(8,128)S(1)}, u32[]{:S(2)}, u32[]{:S(2)}) %collective-permute-start.1) | collective-permute-done | bytes 262176 | tf_op jit(solution)/shard_map/ppermute | solution.py:199
  22.0 0.0 collective-permute-done.2.near
  22.0 1.3 %shard_map.66 = f32[256,128]{1,0:T(8,128)S(1)} custom-call(s32[16]{0:T(128)} %sx.5, s32[16]{0:T(128)} %sy.5, s32[16]{0:T(128)} %sz.5, bf16[512,256]{1,0:T(8,128)(2,1)S(1)} %get-tuple-element.8.parts, f32[4,64,256]{2,1,0:T(8,128)S(1)} %collective-permute-done.1.other, f32[4,64,256]{2,1,0:T(8,128)S(1)} %collective-permute-done.2.near, ...), custom_call_target="tpu_custom_call" | custom-call | tf_op jit(solution)/shard_map/pallas_call | solution.py:191
  23.2 26.3 %all_to_all.11 = f32[256,1,128]{2,1,0:T(1,128)S(1)} all-to-all(f32[256,1,128]{2,1,0:T(1,128)S(1)} %bitcast.5), channel_id=1, replica_groups=mesh['y'=4,'xh'=2,'xl'=2,'z'=8,'c'=2] {'y','xh','xl','z','c'}, dimensions={0} | all-to-all | bytes 262144 | tf_op jit(solution)/shard_map/all_to_all | solution.py:217
  49.5 0.8 %shard_map.67 = f32[3,16]{1,0:T(4,128)} custom-call(f32[256,128]{1,0:T(8,128)S(1)} %bitcast.4), custom_call_target="tpu_custom_call" | custom-call | tf_op jit(solution)/shard_map/pallas_call | solution.py:191
Async XLA Ops:
  0.0 9.9 %copy-start = (f32[8,64,256]{2,1,0:T(8,128)S(1)}, f32[8,64,256]{2,1,0:T(8,128)}, u32[]{:S(2)}) copy-start(f32[8,64,256]{2,1,0:T(8,128)} %v_ref.1) | copy-start | bytes 1572868
  0.0 15.8 %collective-permute-start = (f32[8,64,256]{2,1,0:T(8,128)}, f32[8,64,256]{2,1,0:T(8,128)S(1)}, u32[]{:S(2)}, u32[]{:S(2)}) collective-permute-start(f32[8,64,256]{2,1,0:T(8,128)} %u_ref.1), channel_id=1, source_target_pairs={{0,1},{1,0},{2,3},{3,2},{4,5},{5,4},{6,7},{7,6},{8,9},{9,8},{10,11... | collective-permute-start | bytes 1572872 | tf_op jit(solution)/shard_map/ppermute | solution.py:199
  5.1 14.0 %collective-permute-start.3 = (f32[4,64,256]{2,1,0:T(8,128)}, f32[4,64,256]{2,1,0:T(8,128)S(1)}, u32[]{:S(2)}, u32[]{:S(2)}) collective-permute-start(f32[4,64,256]{2,1,0:T(8,128)} %get-tuple-element.12), channel_id=1, source_target_pairs={{0,30},{1,31},{2,0},{3,1},{4,2},{5,3},{6,4},{7,5},{8,6},{9,7},{10,... | collective-permute-start | bytes 786440 | tf_op jit(solution)/shard_map/ppermute | solution.py:199
  9.9 9.2 %collective-permute-start.4 = (f32[4,64,256]{2,1,0:T(8,128)}, f32[4,64,256]{2,1,0:T(8,128)S(1)}, u32[]{:S(2)}, u32[]{:S(2)}) collective-permute-start(f32[4,64,256]{2,1,0:T(8,128)} %get-tuple-element.11), channel_id=1, source_target_pairs={{0,30},{1,3},{2,0},{3,5},{4,2},{5,7},{6,4},{7,9},{8,6},{9,11},{10,... | collective-permute-start | bytes 786440 | tf_op jit(solution)/shard_map/ppermute | solution.py:199
  10.6 11.3 %collective-permute-start.1 = (f32[4,64,256]{2,1,0:T(8,128)}, f32[4,64,256]{2,1,0:T(8,128)S(1)}, u32[]{:S(2)}, u32[]{:S(2)}) collective-permute-start(f32[4,64,256]{2,1,0:T(8,128)} %get-tuple-element.14), channel_id=1, source_target_pairs={{0,32},{1,33},{2,34},{3,35},{4,36},{5,37},{6,38},{7,39},{8,40},{9,... | collective-permute-start | bytes 786440 | tf_op jit(solution)/shard_map/ppermute | solution.py:199
  13.1 8.9 %collective-permute-start.2 = (f32[4,64,256]{2,1,0:T(8,128)S(1)}, f32[4,64,256]{2,1,0:T(8,128)S(1)}, u32[]{:S(2)}, u32[]{:S(2)}) collective-permute-start(f32[4,64,256]{2,1,0:T(8,128)S(1)} %get-tuple-element.13), channel_id=1, source_target_pairs={{0,192},{1,193},{2,194},{3,195},{4,196},{5,197},{6,198},{7,199},{8... | collective-permute-start | bytes 786440 | tf_op jit(solution)/shard_map/ppermute | solution.py:199

commit v5 on v4

--- a/solution.py
+++ b/solution.py
@@ -13,6 +13,7 @@
 GX = ("xl", "z", "c")
 GY = ("y", "xh")
 F32 = jnp.float32
+UP = 3
 BF16 = jnp.bfloat16
 HIGH = lax.Precision.HIGHEST
 
@@ -38,7 +39,7 @@
     return target
 
 
-U_DOWN = pairs_of(chip_step((-1, -1)))
+U_UP = pairs_of(chip_step((1, 1)))
 U_BOTH = pairs_of(chip_step((-1, 1)))
 U_CORE = pairs_of(lambda y, xh, xl, z, c: (y, xh, xl, z, 1 - c))
 V_SWAP = pairs_of(lambda y, xh, xl, z, c: (y, 1 - xh, xl, z, c))
@@ -101,8 +102,24 @@
     return high, (x - high.astype(F32)).astype(BF16)
 
 
-def own_kernel(sx, sy, sz, u_ref, other, v_ref, w_ref, out_ref, u_parts, v_parts):
+def split_kernel(u_ref, v_ref, up, both, keep, swap, sems):
+    half = lax.axis_index("xh")
+    moves = (
+        (v_ref.at[pl.ds(4 - 4 * half, 4)], swap),
+        (u_ref.at[pl.ds(0, UP)], up),
+        (u_ref.at[pl.ds(UP, 8 - UP)], both),
+        (v_ref.at[pl.ds(4 * half, 4)], keep),
+    )
+    copies = [pltpu.make_async_copy(a, b, sems.at[i]) for i, (a, b) in enumerate(moves)]
+    for copy in copies:
+        copy.start()
+    for copy in copies:
+        copy.wait()
+
+
+def own_kernel(sx, sy, sz, u_ref, other, v_ref, w_ref, lag_ref, out_ref, u_parts, v_parts):
     lags = lag_row((sx, sy, sz))
+    lag_ref[...] = lags
     lane = lane_index()
     half = lax.axis_index("xh")
     grams = jnp.zeros((64, 128), F32)
@@ -134,29 +151,28 @@
     out_ref[...] = jnp.where(of_u, u_sums, jnp.where(of_v, v_sums, w_sums))
 
 
-def u_kernel(sx, sy, sz, parts, near_down, near_both, before, out_ref):
-    lags = lag_row((sx, sy, sz))
+def u_kernel(lag_ref, parts, near_up, near_both, before, out_ref):
+    lags = lag_ref[...]
     first = lax.axis_index("c") == 0
     sums = []
-    for near in (near_down, near_both):
+    for near, planes in ((near_up, range(UP)), (near_both, range(UP, 8))):
         total = jnp.zeros((128, 64), F32)
-        for i in range(4):
-            z = i if near is near_down else 4 + i
-            high, low = halves(near[i])
+        for z in planes:
+            high, low = halves(near[z - planes[0]])
             both = dot_nt(parts[z], high, None)
             total = total + both[:128] + both[128:] + dot_nt(parts[z, :128], low, None)
         sums.append(total)
-    down, mixed = sums
-    far = down[64:] + jnp.where(first, mixed[64:], mixed[64:].T)
-    next_to = jnp.where(first, down[:64] + mixed[:64], 0.0)
+    up, mixed = sums
+    far = jnp.where(first, mixed[64:] + up[64:].T, (mixed[64:] + up[64:]).T)
+    next_to = jnp.where(first, mixed[:64], up[:64].T)
     i = lax.broadcasted_iota(jnp.int32, (64, 64), 0)
     j = lax.broadcasted_iota(jnp.int32, (64, 64), 1)
     gram = jnp.concatenate([next_to, jnp.where(j <= i, far, 0.0)], axis=1)
     out_ref[...] = before[...] + jnp.where(lane_index() < 16, pick(skewed(gram), lags - 64), 0.0)
 
 
-def v_kernel(sx, sy, sz, parts, other, near, before, out_ref):
-    lags = lag_row((sx, sy, sz))
+def v_kernel(lag_ref, parts, other, near, before, out_ref):
+    lags = lag_ref[...]
     lane = lane_index()
     first = lax.axis_index("xh") == 0
     high, low = halves(other[...].reshape(256, 256))
@@ -182,38 +198,47 @@
         out_ref[axis : axis + 1, :] = total[:, axis * 16 : axis * 16 + 16] / energy
 
 
+ROOM = {split_kernel: 2, own_kernel: 16, u_kernel: 12, v_kernel: 12, end_kernel: 4}
 SMEM = pl.BlockSpec(memory_space=pltpu.SMEM)
 VMEM = pl.BlockSpec(memory_space=pltpu.VMEM)
 
 
-def call(kernel, out, *args):
-    specs = [SMEM if a.dtype == jnp.int32 else VMEM for a in args]
-    return pl.pallas_call(kernel, out_shape=out, in_specs=specs, out_specs=jax.tree.map(lambda _: VMEM, out))(*args)
+def call(kernel, out, *args, places=None, **more):
+    places = places or [SMEM if a.dtype == jnp.int32 and a.ndim == 1 else VMEM for a in args]
+    specs = jax.tree.map(lambda _: VMEM, out)
+    room = pltpu.CompilerParams(vmem_limit_bytes=ROOM[kernel] * 2**20)
+    return pl.pallas_call(kernel, out_shape=out, in_specs=places, out_specs=specs, compiler_params=room, **more)(*args)
 
 
 def near(x):
     return pltpu.with_memory_space_constraint(x, pltpu.VMEM)
 
 
+def far(x):
+    return pltpu.with_memory_space_constraint(x, pltpu.HBM)
+
+
 def send(value, pairs):
     return near(lax.ppermute(value, AXES, pairs))
 
 
 def local(u, v, w, sep_x, sep_y, sep_z):
-    half = lax.axis_index("xh")
-    v_keep = lax.dynamic_slice_in_dim(v, 4 * half, 4, 0)
-    v_send = lax.dynamic_slice_in_dim(v, 4 - 4 * half, 4, 0)
+    pieces = [pltpu.VMEM((n, 64, 256), F32) for n in (UP, 8 - UP, 4, 4)]
+    hbm = pl.BlockSpec(memory_space=pltpu.HBM)
+    sems = [pltpu.SemaphoreType.DMA((4,))]
+    made = call(split_kernel, pieces, far(u), far(v), places=[hbm, hbm], scratch_shapes=sems)
+    u_up, u_both, v_keep, v_send = made
     v_other = send(v_send, V_SWAP)
-    down = send(u[:4], U_DOWN)
-    both = send(u[4:], U_BOTH)
+    up = send(u_up, U_UP)
+    both = send(u_both, U_BOTH)
     u_other = send(u, U_CORE)
     v_near = send(v_keep, V_NEXT)
-    seps = (sep_x, sep_y, sep_z)
     row = pltpu.VMEM((8, 128), F32)
-    outs = (row, pltpu.VMEM((8, 256, 256), BF16), pltpu.VMEM((512, 256), BF16))
-    part, u_parts, v_parts = call(own_kernel, outs, *seps, u, u_other, v, w)
-    part = call(u_kernel, row, *seps, near(u_parts), down, both, near(part))
-    rows = call(v_kernel, pltpu.VMEM((256, 128), F32), *seps, near(v_parts), v_other, v_near, near(part))
+    outs = (pltpu.VMEM((8, 128), jnp.int32), row, pltpu.VMEM((8, 256, 256), BF16), pltpu.VMEM((512, 256), BF16))
+    made = call(own_kernel, outs, sep_x, sep_y, sep_z, u, u_other, v, w)
+    lags, part, u_parts, v_parts = map(near, made)
+    part = call(u_kernel, row, lags, u_parts, up, both, part)
+    rows = call(v_kernel, pltpu.VMEM((256, 128), F32), lags, v_parts, v_other, v_near, near(part))
     rows = near(lax.all_to_all(rows, SERVED, 0, 0, tiled=True))
     return call(end_kernel, jax.ShapeDtypeStruct((3, 16), F32), rows)
 

time: 50.4 us -> 44.2 us (0.88)
  starting transfers between devices: 13.2 us -> 10.3 us
  blocking collectives: 26.3 us -> 24.4 us
  local copies, waits for them, and re-layouts: 2.6 us -> 1.06 us
  Pallas kernels: 6.87 us -> 6 us
  waiting for transfers between devices: 1.32 us -> 2.18 us
    ppermute x5, starting transfers between devices: 13.2 us -> 10.3 us  [send(): return near(lax.ppermute(value, AXES, pairs))]
    all_to_all x1, blocking collectives: 26.3 us -> 24.4 us  [local(): rows = near(lax.all_to_all(rows, SERVED, 0, 0, tiled=True))]
    slice x1 -> x0, local copies, waits for them, and re-layouts: 1.87 us -> none  [local(): both = send(u[4:], U_BOTH)]
    unnamed x2 -> x12, local copies, waits for them, and re-layouts: 0.01 us -> 1.06 us
    pallas_call x4 -> x5, Pallas kernels: 6.87 us -> 6 us  [call(): pl.pallas_call(kernel, out_shape=out, in_specs=places, out_specs=specs, c...]
    ppermute x5, waiting for transfers between devices: 1.32 us -> 2.18 us  [send(): return near(lax.ppermute(value, AXES, pairs))]
    dynamic_slice x1 -> x0, local copies, waits for them, and re-layouts: 0.73 us -> none  [local(): v_keep = lax.dynamic_slice_in_dim(v, 4 * half, 4, 0)]
  transfers between devices with their start and end apart: 5 -> 5, of which waited for: 1 -> 1; matrix products, arithmetic and copies ran while one was open for 5% -> 0% of each run, Pallas kernels for 10% -> 11%
where the time goes in v5:
time: 44.2 us; the launch traced here: 44 us
  blocking collectives  24.4 us (55%)
  starting transfers between devices  10.3 us (23%)
  Pallas kernels  6 us (14%)
  waiting for transfers between devices  2.18 us (5%)
  local copies, waits for them, and re-layouts  1.06 us (2%)
    all_to_all x1, blocking collectives, local(): rows = near(lax.all_to_all(rows, SERVED, 0, 0, tiled=True))  24.4 us
    ppermute x5, starting transfers between devices, send(): return near(lax.ppermute(value, AXES, pairs))  10.3 us
    pallas_call x5, Pallas kernels, call(): pl.pallas_call(kernel, out_shape=out, in_specs=places, out_specs=specs, c...  6 us
    ppermute x5, waiting for transfers between devices, send(): return near(lax.ppermute(value, AXES, pairs))  2.18 us
    unnamed x12, local copies, waits for them, and re-layouts  1.06 us
  transfers between devices with their start and end apart: 5, of which 1 were waited for; matrix products, arithmetic and copies ran while one was open for 0% of the time, Pallas kernels for 11%

profile of v5, /device:TPU:1, one launch (start us, length us, event | category | flops | bytes accessed | tf_op | source)
XLA Modules:
  0.0 44.0 jit_solution(4998729435476859076)
XLA Ops:
  0.0 0.0 copy-start
  0.0 3.2 %collective-permute-start = (f32[8,64,256]{2,1,0:T(8,128)}, f32[8,64,256]{2,1,0:T(8,128)S(1)}, u32[]{:S(2)}, u32[]{:S(2)}) collective-permute-start(f32[8,64,256]{2,1,0:T(8,128)} %u_ref.3), channel_id=1, source_target_pairs={{0,1},{1,0},{2,3},{3,2},{4,5},{5,4},{6,7},{7,6},{8,9},{9,8},{10,11... | collective-permute-start | bytes 1572872 | tf_op jit(solution)/shard_map/ppermute | solution.py:222
  3.2 1.3 %shard_map.65 = (f32[3,64,256]{2,1,0:T(8,128)S(1)}, f32[5,64,256]{2,1,0:T(8,128)S(1)}, f32[4,64,256]{2,1,0:T(8,128)S(1)}, f32[4,64,256]{2,1,0:T(8,128)S(1)}) custom-call(f32[8,64,256]{2,1,0:T(8,128)} %u_ref.3, f32[8,64,256]{2,1,0:T(8,128)} %v_ref.3), custom_call_target="tpu_custom_call" | custom-call | tf_op jit(solution)/shard_map/pallas_call | solution.py:210
  4.5 0.1 collective-permute-start.4
  4.6 2.7 %collective-permute-start.1 = (f32[4,64,256]{2,1,0:T(8,128)S(1)}, f32[4,64,256]{2,1,0:T(8,128)S(1)}, u32[]{:S(2)}, u32[]{:S(2)}) collective-permute-start(f32[4,64,256]{2,1,0:T(8,128)S(1)} %get-tuple-element.15), channel_id=1, source_target_pairs={{0,32},{1,33},{2,34},{3,35},{4,36},{5,37},{6,38},{7,39},{8,40},{9,... | collective-permute-start | bytes 786440 | tf_op jit(solution)/shard_map/ppermute | solution.py:222
  7.2 2.7 %collective-permute-start.2 = (f32[4,64,256]{2,1,0:T(8,128)S(1)}, f32[4,64,256]{2,1,0:T(8,128)S(1)}, u32[]{:S(2)}, u32[]{:S(2)}) collective-permute-start(f32[4,64,256]{2,1,0:T(8,128)S(1)} %get-tuple-element.16), channel_id=1, source_target_pairs={{0,192},{1,193},{2,194},{3,195},{4,196},{5,197},{6,198},{7,199},{8... | collective-permute-start | bytes 786440 | tf_op jit(solution)/shard_map/ppermute | solution.py:222
  10.0 1.6 %collective-permute-start.3 = (f32[3,64,256]{2,1,0:T(8,128)S(1)}, f32[3,64,256]{2,1,0:T(8,128)S(1)}, u32[]{:S(2)}, u32[]{:S(2)}) collective-permute-start(f32[3,64,256]{2,1,0:T(8,128)S(1)} %get-tuple-element.18), channel_id=1, source_target_pairs={{0,2},{1,3},{2,4},{3,5},{4,6},{5,7},{6,8},{7,9},{8,10},{9,11},{10,... | collective-permute-start | bytes 589832 | tf_op jit(solution)/shard_map/ppermute | solution.py:222
  11.6 0.0 collective-permute-done.other
  11.6 0.0 copy-done
  11.6 0.0 copy-done.1
  11.6 0.0 copy-done.3
  11.6 0.0 copy-done.4
  11.6 0.0 copy-done.5
  11.6 0.0 copy-start.2
  11.7 1.0 %copy-done.2 = f32[8,64,256]{2,1,0:T(8,128)S(1)} copy-done((f32[8,64,256]{2,1,0:T(8,128)S(1)}, f32[8,64,256]{2,1,0:T(8,128)}, u32[]{:S(2)}) %copy-start.2) | copy-done | bytes 524312
  12.7 2.5 %shard_map.64 = (s32[8,128]{1,0:T(8,128)S(1)}, f32[8,128]{1,0:T(8,128)S(1)}, bf16[8,256,256]{2,1,0:T(8,128)(2,1)S(1)}, bf16[512,256]{1,0:T(8,128)(2,1)S(1)}) custom-call(s32[16]{0:T(128)S(1)} %copy-done.3, s32[16]{0:T(128)S(1)} %copy-done.4, s32[16]{0:T(128)S(1)} %copy-done.5, f32[8,64,256]{2,1,0:T(8,128)S(1)} %copy-done, ...), custom_call_target="tpu_custom_call" | custom-call | tf_op jit(solution)/shard_map/pallas_call | solution.py:210
  15.2 2.2 %collective-permute-done.3.near_up = f32[3,64,256]{2,1,0:T(8,128)S(1)} collective-permute-done((f32[3,64,256]{2,1,0:T(8,128)S(1)}, f32[3,64,256]{2,1,0:T(8,128)S(1)}, u32[]{:S(2)}, u32[]{:S(2)}) %collective-permute-start.3) | collective-permute-done | bytes 196640 | tf_op jit(solution)/shard_map/ppermute | solution.py:222
  17.4 0.0 collective-permute-done.4.near_both
  17.4 0.9 %shard_map.66.before = f32[8,128]{1,0:T(8,128)S(1)} custom-call(s32[8,128]{1,0:T(8,128)S(1)} %get-tuple-element.13.lag_ref, bf16[8,256,256]{2,1,0:T(8,128)(2,1)S(1)} %get-tuple-element.17.parts, f32[3,64,256]{2,1,0:T(8,128)S(1)} %collective-permute-done.3.near_up, f32[5,64,256]{2,1,0:T(8,128)S(1)} %collective-permute-done.4.near_both, ...), custom_call_target="tpu_custom_call" | custom-call | tf_op jit(solution)/shard_map/pallas_call | solution.py:210
  18.2 0.0 collective-permute-done.1.other
  18.3 0.0 collective-permute-done.2.near
  18.3 0.6 %shard_map.67 = f32[256,128]{1,0:T(8,128)S(1)} custom-call(s32[8,128]{1,0:T(8,128)S(1)} %get-tuple-element.13.lag_ref, bf16[512,256]{1,0:T(8,128)(2,1)S(1)} %get-tuple-element.14.parts, f32[4,64,256]{2,1,0:T(8,128)S(1)} %collective-permute-done.1.other, f32[4,64,256]{2,1,0:T(8,128)S(1)} %collective-permute-done.2.near, f32[8,128]{1,0:T(8,128)S(1)} %shard_map.66.before), custom_call_target="tpu_custom_call" | custom-call | tf_op jit(solution)/shard_map/pallas_call | solution.py:210
  18.9 24.4 %all_to_all.11 = f32[256,1,128]{2,1,0:T(1,128)S(1)} all-to-all(f32[256,1,128]{2,1,0:T(1,128)S(1)} %bitcast.4), channel_id=1, replica_groups=mesh['y'=4,'xh'=2,'xl'=2,'z'=8,'c'=2] {'y','xh','xl','z','c'}, dimensions={0} | all-to-all | bytes 262144 | tf_op jit(solution)/shard_map/all_to_all | solution.py:242
  43.2 0.8 %shard_map.68 = f32[3,16]{1,0:T(4,128)} custom-call(f32[256,128]{1,0:T(8,128)S(1)} %bitcast.5), custom_call_target="tpu_custom_call" | custom-call | tf_op jit(solution)/shard_map/pallas_call | solution.py:210
  (4 shorter events, 0.0 us)
Async XLA Ops:
  0.0 11.6 %copy-start = (f32[8,64,256]{2,1,0:T(8,128)S(1)}, f32[8,64,256]{2,1,0:T(8,128)}, u32[]{:S(2)}) copy-start(f32[8,64,256]{2,1,0:T(8,128)} %u_ref.3) | copy-start | bytes 1572868
  0.0 11.6 %copy-start.1 = (f32[8,64,256]{2,1,0:T(8,128)S(1)}, f32[8,64,256]{2,1,0:T(8,128)}, u32[]{:S(2)}) copy-start(f32[8,64,256]{2,1,0:T(8,128)} %v_ref.3) | copy-start | bytes 1572868
  0.0 11.6 %collective-permute-start = (f32[8,64,256]{2,1,0:T(8,128)}, f32[8,64,256]{2,1,0:T(8,128)S(1)}, u32[]{:S(2)}, u32[]{:S(2)}) collective-permute-start(f32[8,64,256]{2,1,0:T(8,128)} %u_ref.3), channel_id=1, source_target_pairs={{0,1},{1,0},{2,3},{3,2},{4,5},{5,4},{6,7},{7,6},{8,9},{9,8},{10,11... | collective-permute-start | bytes 1572872 | tf_op jit(solution)/shard_map/ppermute | solution.py:222
  4.5 12.9 %collective-permute-start.4 = (f32[5,64,256]{2,1,0:T(8,128)S(1)}, f32[5,64,256]{2,1,0:T(8,128)S(1)}, u32[]{:S(2)}, u32[]{:S(2)}) collective-permute-start(f32[5,64,256]{2,1,0:T(8,128)S(1)} %get-tuple-element.19), channel_id=1, source_target_pairs={{0,30},{1,3},{2,0},{3,5},{4,2},{5,7},{6,4},{7,9},{8,6},{9,11},{10,... | collective-permute-start | bytes 983048 | tf_op jit(solution)/shard_map/ppermute | solution.py:222
  4.6 13.7 %collective-permute-start.1 = (f32[4,64,256]{2,1,0:T(8,128)S(1)}, f32[4,64,256]{2,1,0:T(8,128)S(1)}, u32[]{:S(2)}, u32[]{:S(2)}) collective-permute-start(f32[4,64,256]{2,1,0:T(8,128)S(1)} %get-tuple-element.15), channel_id=1, source_target_pairs={{0,32},{1,33},{2,34},{3,35},{4,36},{5,37},{6,38},{7,39},{8,40},{9,... | collective-permute-start | bytes 786440 | tf_op jit(solution)/shard_map/ppermute | solution.py:222
  7.2 4.4 %copy-start.3 = (s32[16]{0:T(128)S(1)}, s32[16]{0:T(128)}, u32[]{:S(2)}) copy-start(s32[16]{0:T(128)} %sx.1) | copy-start | bytes 196
  7.2 4.4 %copy-start.4 = (s32[16]{0:T(128)S(1)}, s32[16]{0:T(128)}, u32[]{:S(2)}) copy-start(s32[16]{0:T(128)} %sy.1) | copy-start | bytes 196
  7.2 4.4 %copy-start.5 = (s32[16]{0:T(128)S(1)}, s32[16]{0:T(128)}, u32[]{:S(2)}) copy-start(s32[16]{0:T(128)} %sz.1) | copy-start | bytes 196
  7.2 11.0 %collective-permute-start.2 = (f32[4,64,256]{2,1,0:T(8,128)S(1)}, f32[4,64,256]{2,1,0:T(8,128)S(1)}, u32[]{:S(2)}, u32[]{:S(2)}) collective-permute-start(f32[4,64,256]{2,1,0:T(8,128)S(1)} %get-tuple-element.16), channel_id=1, source_target_pairs={{0,192},{1,193},{2,194},{3,195},{4,196},{5,197},{6,198},{7,199},{8... | collective-permute-start | bytes 786440 | tf_op jit(solution)/shard_map/ppermute | solution.py:222
  10.0 7.4 %collective-permute-start.3 = (f32[3,64,256]{2,1,0:T(8,128)S(1)}, f32[3,64,256]{2,1,0:T(8,128)S(1)}, u32[]{:S(2)}, u32[]{:S(2)}) collective-permute-start(f32[3,64,256]{2,1,0:T(8,128)S(1)} %get-tuple-element.18), channel_id=1, source_target_pairs={{0,2},{1,3},{2,4},{3,5},{4,6},{5,7},{6,8},{7,9},{8,10},{9,11},{10,... | collective-permute-start | bytes 589832 | tf_op jit(solution)/shard_map/ppermute | solution.py:222
  11.6 1.0 %copy-start.2 = (f32[8,64,256]{2,1,0:T(8,128)S(1)}, f32[8,64,256]{2,1,0:T(8,128)}, u32[]{:S(2)}) copy-start(f32[8,64,256]{2,1,0:T(8,128)} %w_ref.1) | copy-start | bytes 1572868

commit v6 on v5

--- a/solution.py
+++ b/solution.py
@@ -117,26 +117,23 @@
         copy.wait()
 
 
-def own_kernel(sx, sy, sz, u_ref, other, v_ref, w_ref, lag_ref, out_ref, u_parts, v_parts):
+def own_kernel(sx, sy, sz, u_up, u_both, keep, swap, w_far, lag_ref, out_ref, v_parts, w_ref, sem):
+    fetch = pltpu.make_async_copy(w_far, w_ref, sem)
+    fetch.start()
     lags = lag_row((sx, sy, sz))
     lag_ref[...] = lags
     lane = lane_index()
-    half = lax.axis_index("xh")
-    grams = jnp.zeros((64, 128), F32)
-    for z in range(8):
-        a, b = u_ref[z], other[z]
-        grams = grams + dot_nt(a, jnp.concatenate([a, b], axis=0))
-        a_high, a_low = halves(a)
-        b_high, b_low = halves(b)
-        u_parts[z] = jnp.concatenate([b_high, a_high, b_low, a_low], axis=0)
-    u_sums = jnp.where(lags < 64, pick(skewed(widened(grams[:, :64])), lags), 0.0)
-    cores = pick(skewed(widened(grams[:, 64:])), 64 - lags)
-    counted = (lax.axis_index("c") == 1) & (lags > 0) & (lags < 128)
-    u_sums = u_sums + jnp.where(counted, cores, 0.0)
-    keep = v_ref[pl.ds(4 * half, 4)].reshape(256, 256).T
-    v_parts[:256], v_parts[256:] = halves(keep)
-    v_rows = v_ref[...].reshape(512, 256)
-    v_sums = pick(skewed(widened(dot_tn(v_rows, v_rows))), lags)
+    gram = jnp.zeros((64, 128), F32)
+    pad = jnp.zeros((64, 256), F32)
+    for piece in (u_up, u_both):
+        for z in range(piece.shape[0]):
+            gram = gram + dot_nt(piece[z], jnp.concatenate([piece[z], pad], axis=0))
+    u_sums = jnp.where(lags < 64, pick(skewed(gram), lags), 0.0)
+    kept = keep[...].reshape(256, 256)
+    sent = swap[...].reshape(256, 256)
+    v_parts[:256], v_parts[256:] = halves(kept.T)
+    v_sums = pick(skewed(widened(dot_tn(kept, kept) + dot_tn(sent, sent))), lags)
+    fetch.wait()
     planes = [w_ref[z] for z in range(8)]
     w_sums = jnp.zeros((8, 128), F32)
     for lag in range(5):
@@ -149,6 +146,18 @@
     of_u = (lane < 16) | (lane == 48)
     of_v = (lane < 32) | (lane == 49)
     out_ref[...] = jnp.where(of_u, u_sums, jnp.where(of_v, v_sums, w_sums))
+
+
+def core_kernel(lag_ref, u_up, u_both, other_up, other_both, before, out_ref, u_parts):
+    lags = lag_ref[...]
+    gram = jnp.zeros((64, 64), F32)
+    for z in range(8):
+        a_high, a_low = halves(u_up[z] if z < UP else u_both[z - UP])
+        b_high, b_low = halves(other_up[z] if z < UP else other_both[z - UP])
+        u_parts[z] = jnp.concatenate([b_high, a_high, b_low, a_low], axis=0)
+        gram = gram + dot_nt(b_high, a_high, None) + dot_nt(b_low, a_high, None) + dot_nt(b_high, a_low, None)
+    counted = (lax.axis_index("c") == 1) & (lane_index() < 16) & (lags < 128)
+    out_ref[...] = before[...] + jnp.where(counted, pick(skewed(widened(gram)), lags - 64), 0.0)
 
 
 def u_kernel(lag_ref, parts, near_up, near_both, before, out_ref):
@@ -198,7 +207,7 @@
         out_ref[axis : axis + 1, :] = total[:, axis * 16 : axis * 16 + 16] / energy
 
 
-ROOM = {split_kernel: 2, own_kernel: 16, u_kernel: 12, v_kernel: 12, end_kernel: 4}
+ROOM = {core_kernel: 12, split_kernel: 2, own_kernel: 16, u_kernel: 12, v_kernel: 12, end_kernel: 4}
 SMEM = pl.BlockSpec(memory_space=pltpu.SMEM)
 VMEM = pl.BlockSpec(memory_space=pltpu.VMEM)
 
@@ -231,12 +240,17 @@
     v_other = send(v_send, V_SWAP)
     up = send(u_up, U_UP)
     both = send(u_both, U_BOTH)
-    u_other = send(u, U_CORE)
+    other_up = send(u_up, U_CORE)
+    other_both = send(u_both, U_CORE)
     v_near = send(v_keep, V_NEXT)
     row = pltpu.VMEM((8, 128), F32)
-    outs = (pltpu.VMEM((8, 128), jnp.int32), row, pltpu.VMEM((8, 256, 256), BF16), pltpu.VMEM((512, 256), BF16))
-    made = call(own_kernel, outs, sep_x, sep_y, sep_z, u, u_other, v, w)
-    lags, part, u_parts, v_parts = map(near, made)
+    outs = (pltpu.VMEM((8, 128), jnp.int32), row, pltpu.VMEM((512, 256), BF16))
+    args = (sep_x, sep_y, sep_z, *map(near, (u_up, u_both, v_keep, v_send)), far(w))
+    places = [SMEM] * 3 + [VMEM] * 4 + [hbm]
+    scratch = [pltpu.VMEM((8, 64, 256), F32), pltpu.SemaphoreType.DMA]
+    lags, part, v_parts = map(near, call(own_kernel, outs, *args, places=places, scratch_shapes=scratch))
+    outs = (row, pltpu.VMEM((8, 256, 256), BF16))
+    part, u_parts = map(near, call(core_kernel, outs, lags, near(u_up), near(u_both), other_up, other_both, part))
     part = call(u_kernel, row, lags, u_parts, up, both, part)
     rows = call(v_kernel, pltpu.VMEM((256, 128), F32), lags, v_parts, v_other, v_near, near(part))
     rows = near(lax.all_to_all(rows, SERVED, 0, 0, tiled=True))

time: 44.2 us -> 44.3 us (level)
  local copies, waits for them, and re-layouts: 1.06 us -> 0.01 us
  Pallas kernels: 6 us -> 6.92 us
    unnamed x12 -> x6, local copies, waits for them, and re-layouts: 1.06 us -> 0.01 us
    pallas_call x5 -> x6, Pallas kernels: 6 us -> 6.92 us  [call(): pl.pallas_call(kernel, out_shape=out, in_specs=places, out_specs=specs, c...]
    ppermute x5 -> x6, waiting for transfers between devices: 2.18 us -> 2.33 us  [send(): return near(lax.ppermute(value, AXES, pairs))]
    ppermute x5 -> x6, starting transfers between devices: 10.3 us -> 10.4 us  [send(): return near(lax.ppermute(value, AXES, pairs))]
  transfers between devices with their start and end apart: 5 -> 6, of which waited for: 1 -> 1; matrix products, arithmetic and copies ran while one was open for 0% -> 0% of each run, Pallas kernels for 11% -> 10%
where the time goes in v6:
time: 44.3 us; the launch traced here: 44.1 us
  blocking collectives  24.4 us (55%)
  starting transfers between devices  10.4 us (23%)
  Pallas kernels  6.92 us (16%)
  waiting for transfers between devices  2.33 us (5%)
    all_to_all x1, blocking collectives, local(): rows = near(lax.all_to_all(rows, SERVED, 0, 0, tiled=True))  24.4 us
    ppermute x6, starting transfers between devices, send(): return near(lax.ppermute(value, AXES, pairs))  10.4 us
    pallas_call x6, Pallas kernels, call(): pl.pallas_call(kernel, out_shape=out, in_specs=places, out_specs=specs, c...  6.92 us
    ppermute x6, waiting for transfers between devices, send(): return near(lax.ppermute(value, AXES, pairs))  2.33 us
  transfers between devices with their start and end apart: 6, of which 1 were waited for; matrix products, arithmetic and copies ran while one was open for 0% of the time, Pallas kernels for 10%

profile of v6, /device:TPU:1, one launch (start us, length us, event | category | flops | bytes accessed | tf_op | source)
XLA Modules:
  0.0 44.1 jit_solution(899433676522607015)
XLA Ops:
  0.0 1.3 %shard_map.64 = (f32[3,64,256]{2,1,0:T(8,128)S(1)}, f32[5,64,256]{2,1,0:T(8,128)S(1)}, f32[4,64,256]{2,1,0:T(8,128)S(1)}, f32[4,64,256]{2,1,0:T(8,128)S(1)}) custom-call(f32[8,64,256]{2,1,0:T(8,128)} %u_ref.1, f32[8,64,256]{2,1,0:T(8,128)} %v_ref.1), custom_call_target="tpu_custom_call" | custom-call | tf_op jit(solution)/shard_map/pallas_call | solution.py:219
  1.3 3.3 %collective-permute-start.2 = (f32[3,64,256]{2,1,0:T(8,128)S(1)}, f32[3,64,256]{2,1,0:T(8,128)S(1)}, u32[]{:S(2)}, u32[]{:S(2)}) collective-permute-start(f32[3,64,256]{2,1,0:T(8,128)S(1)} %get-tuple-element.14.u_up), channel_id=1, source_target_pairs={{0,1},{1,0},{2,3},{3,2},{4,5},{5,4},{6,7},{7,6},{8,9},{9,8},{10,11... | collective-permute-start | bytes 589832 | tf_op jit(solution)/shard_map/ppermute | solution.py:231
  4.6 0.1 collective-permute-start.3
  4.7 0.0 collective-permute-start.5
  4.7 0.0 copy-start
  4.7 0.0 copy-start.2
  4.7 2.7 %collective-permute-start = (f32[4,64,256]{2,1,0:T(8,128)S(1)}, f32[4,64,256]{2,1,0:T(8,128)S(1)}, u32[]{:S(2)}, u32[]{:S(2)}) collective-permute-start(f32[4,64,256]{2,1,0:T(8,128)S(1)} %get-tuple-element.17.swap), channel_id=1, source_target_pairs={{0,32},{1,33},{2,34},{3,35},{4,36},{5,37},{6,38},{7,39},{8,40},{9,... | collective-permute-start | bytes 786440 | tf_op jit(solution)/shard_map/ppermute | solution.py:231
  7.3 2.7 %collective-permute-start.1 = (f32[4,64,256]{2,1,0:T(8,128)S(1)}, f32[4,64,256]{2,1,0:T(8,128)S(1)}, u32[]{:S(2)}, u32[]{:S(2)}) collective-permute-start(f32[4,64,256]{2,1,0:T(8,128)S(1)} %get-tuple-element.16.keep), channel_id=1, source_target_pairs={{0,192},{1,193},{2,194},{3,195},{4,196},{5,197},{6,198},{7,199},{8... | collective-permute-start | bytes 786440 | tf_op jit(solution)/shard_map/ppermute | solution.py:231
  10.1 0.0 collective-permute-done.2.other_up
  10.1 1.6 %collective-permute-start.4 = (f32[3,64,256]{2,1,0:T(8,128)S(1)}, f32[3,64,256]{2,1,0:T(8,128)S(1)}, u32[]{:S(2)}, u32[]{:S(2)}) collective-permute-start(f32[3,64,256]{2,1,0:T(8,128)S(1)} %get-tuple-element.14.u_up), channel_id=1, source_target_pairs={{0,2},{1,3},{2,4},{3,5},{4,6},{5,7},{6,8},{7,9},{8,10},{9,11},{10,... | collective-permute-start | bytes 589832 | tf_op jit(solution)/shard_map/ppermute | solution.py:231
  11.7 0.0 copy-done
  11.7 0.0 copy-done.1
  11.7 0.0 copy-done.2
  11.7 2.9 %shard_map.65 = (s32[8,128]{1,0:T(8,128)S(1)}, f32[8,128]{1,0:T(8,128)S(1)}, bf16[512,256]{1,0:T(8,128)(2,1)S(1)}) custom-call(s32[16]{0:T(128)S(1)} %copy-done, s32[16]{0:T(128)S(1)} %copy-done.1, s32[16]{0:T(128)S(1)} %copy-done.2, f32[3,64,256]{2,1,0:T(8,128)S(1)} %get-tuple-element.14.u_up, f32[5,64,256]{2,1,0:T(8,128)S(1)} %get-tuple-element.15.u_both, ...), custom_call_target="tpu_custom_call" | custom-call | tf_op jit(solution)/shard_map/pallas_call | solution.py:219
  14.6 0.0 collective-permute-done.3.other_both
  14.6 0.6 %shard_map.66 = (f32[8,128]{1,0:T(8,128)S(1)}, bf16[8,256,256]{2,1,0:T(8,128)(2,1)S(1)}) custom-call(s32[8,128]{1,0:T(8,128)S(1)} %get-tuple-element.18.lag_ref, f32[3,64,256]{2,1,0:T(8,128)S(1)} %get-tuple-element.14.u_up, f32[5,64,256]{2,1,0:T(8,128)S(1)} %get-tuple-element.15.u_both, f32[3,64,256]{2,1,0:T(8,128)S(1)} %collective-permute-done.2.other_up, ...), custom_call_target="tpu_custom_call" | custom-call | tf_op jit(solution)/shard_map/pallas_call | solution.py:219
  15.2 2.3 %collective-permute-done.4.near_up = f32[3,64,256]{2,1,0:T(8,128)S(1)} collective-permute-done((f32[3,64,256]{2,1,0:T(8,128)S(1)}, f32[3,64,256]{2,1,0:T(8,128)S(1)}, u32[]{:S(2)}, u32[]{:S(2)}) %collective-permute-start.4) | collective-permute-done | bytes 196640 | tf_op jit(solution)/shard_map/ppermute | solution.py:231
  17.5 0.0 collective-permute-done.5.near_both
  17.5 0.9 %shard_map.67.before = f32[8,128]{1,0:T(8,128)S(1)} custom-call(s32[8,128]{1,0:T(8,128)S(1)} %get-tuple-element.18.lag_ref, bf16[8,256,256]{2,1,0:T(8,128)(2,1)S(1)} %get-tuple-element.21.parts, f32[3,64,256]{2,1,0:T(8,128)S(1)} %collective-permute-done.4.near_up, f32[5,64,256]{2,1,0:T(8,128)S(1)} %collective-permute-done.5.near_both, ...), custom_call_target="tpu_custom_call" | custom-call | tf_op jit(solution)/shard_map/pallas_call | solution.py:219
  18.4 0.0 collective-permute-done.other
  18.4 0.0 collective-permute-done.1.near
  18.4 0.6 %shard_map.68 = f32[256,128]{1,0:T(8,128)S(1)} custom-call(s32[8,128]{1,0:T(8,128)S(1)} %get-tuple-element.18.lag_ref, bf16[512,256]{1,0:T(8,128)(2,1)S(1)} %get-tuple-element.19.parts, f32[4,64,256]{2,1,0:T(8,128)S(1)} %collective-permute-done.other, f32[4,64,256]{2,1,0:T(8,128)S(1)} %collective-permute-done.1.near, f32[8,128]{1,0:T(8,128)S(1)} %shard_map.67.before), custom_call_target="tpu_custom_call" | custom-call | tf_op jit(solution)/shard_map/pallas_call | solution.py:219
  19.0 24.4 %all_to_all.11 = f32[256,1,128]{2,1,0:T(1,128)S(1)} all-to-all(f32[256,1,128]{2,1,0:T(1,128)S(1)} %bitcast.4), channel_id=1, replica_groups=mesh['y'=4,'xh'=2,'xl'=2,'z'=8,'c'=2] {'y','xh','xl','z','c'}, dimensions={0} | all-to-all | bytes 262144 | tf_op jit(solution)/shard_map/all_to_all | solution.py:256
  43.4 0.8 %shard_map.69 = f32[3,16]{1,0:T(4,128)} custom-call(f32[256,128]{1,0:T(8,128)S(1)} %bitcast.5), custom_call_target="tpu_custom_call" | custom-call | tf_op jit(solution)/shard_map/pallas_call | solution.py:219
  (1 shorter events, 0.0 us)
Async XLA Ops:
  1.3 8.8 %collective-permute-start.2 = (f32[3,64,256]{2,1,0:T(8,128)S(1)}, f32[3,64,256]{2,1,0:T(8,128)S(1)}, u32[]{:S(2)}, u32[]{:S(2)}) collective-permute-start(f32[3,64,256]{2,1,0:T(8,128)S(1)} %get-tuple-element.14.u_up), channel_id=1, source_target_pairs={{0,1},{1,0},{2,3},{3,2},{4,5},{5,4},{6,7},{7,6},{8,9},{9,8},{10,11... | collective-permute-start | bytes 589832 | tf_op jit(solution)/shard_map/ppermute | solution.py:231
  4.6 10.0 %collective-permute-start.3 = (f32[5,64,256]{2,1,0:T(8,128)S(1)}, f32[5,64,256]{2,1,0:T(8,128)S(1)}, u32[]{:S(2)}, u32[]{:S(2)}) collective-permute-start(f32[5,64,256]{2,1,0:T(8,128)S(1)} %get-tuple-element.15.u_both), channel_id=1, source_target_pairs={{0,1},{1,0},{2,3},{3,2},{4,5},{5,4},{6,7},{7,6},{8,9},{9,8},{10,11... | collective-permute-start | bytes 983048 | tf_op jit(solution)/shard_map/ppermute | solution.py:231
  4.7 12.8 %collective-permute-start.5 = (f32[5,64,256]{2,1,0:T(8,128)S(1)}, f32[5,64,256]{2,1,0:T(8,128)S(1)}, u32[]{:S(2)}, u32[]{:S(2)}) collective-permute-start(f32[5,64,256]{2,1,0:T(8,128)S(1)} %get-tuple-element.15.u_both), channel_id=1, source_target_pairs={{0,30},{1,3},{2,0},{3,5},{4,2},{5,7},{6,4},{7,9},{8,6},{9,11},{10,... | collective-permute-start | bytes 983048 | tf_op jit(solution)/shard_map/ppermute | solution.py:231
  4.7 7.1 %copy-start = (s32[16]{0:T(128)S(1)}, s32[16]{0:T(128)}, u32[]{:S(2)}) copy-start(s32[16]{0:T(128)} %sx.1) | copy-start | bytes 196
  4.7 7.1 %copy-start.1 = (s32[16]{0:T(128)S(1)}, s32[16]{0:T(128)}, u32[]{:S(2)}) copy-start(s32[16]{0:T(128)} %sy.1) | copy-start | bytes 196
  4.7 7.1 %copy-start.2 = (s32[16]{0:T(128)S(1)}, s32[16]{0:T(128)}, u32[]{:S(2)}) copy-start(s32[16]{0:T(128)} %sz.1) | copy-start | bytes 196
  4.7 13.7 %collective-permute-start = (f32[4,64,256]{2,1,0:T(8,128)S(1)}, f32[4,64,256]{2,1,0:T(8,128)S(1)}, u32[]{:S(2)}, u32[]{:S(2)}) collective-permute-start(f32[4,64,256]{2,1,0:T(8,128)S(1)} %get-tuple-element.17.swap), channel_id=1, source_target_pairs={{0,32},{1,33},{2,34},{3,35},{4,36},{5,37},{6,38},{7,39},{8,40},{9,... | collective-permute-start | bytes 786440 | tf_op jit(solution)/shard_map/ppermute | solution.py:231
  7.3 11.0 %collective-permute-start.1 = (f32[4,64,256]{2,1,0:T(8,128)S(1)}, f32[4,64,256]{2,1,0:T(8,128)S(1)}, u32[]{:S(2)}, u32[]{:S(2)}) collective-permute-start(f32[4,64,256]{2,1,0:T(8,128)S(1)} %get-tuple-element.16.keep), channel_id=1, source_target_pairs={{0,192},{1,193},{2,194},{3,195},{4,196},{5,197},{6,198},{7,199},{8... | collective-permute-start | bytes 786440 | tf_op jit(solution)/shard_map/ppermute | solution.py:231
  10.1 7.4 %collective-permute-start.4 = (f32[3,64,256]{2,1,0:T(8,128)S(1)}, f32[3,64,256]{2,1,0:T(8,128)S(1)}, u32[]{:S(2)}, u32[]{:S(2)}) collective-permute-start(f32[3,64,256]{2,1,0:T(8,128)S(1)} %get-tuple-element.14.u_up), channel_id=1, source_target_pairs={{0,2},{1,3},{2,4},{3,5},{4,6},{5,7},{6,8},{7,9},{8,10},{9,11},{10,... | collective-permute-start | bytes 589832 | tf_op jit(solution)/shard_map/ppermute | solution.py:231

commit v7 on v6

--- a/solution.py
+++ b/solution.py
@@ -15,7 +15,6 @@
 F32 = jnp.float32
 UP = 3
 BF16 = jnp.bfloat16
-HIGH = lax.Precision.HIGHEST
 
 
 def pairs_of(target):
@@ -46,12 +45,8 @@
 V_NEXT = pairs_of(lambda y, xh, xl, z, c: (y + (1 if xh else -1), xh, xl, z, c))
 
 
-def dot_nt(a, b, precision=HIGH):
-    return lax.dot_general(a, b, (((1,), (1,)), ((), ())), precision=precision, preferred_element_type=F32)
-
-
-def dot_tn(a, b):
-    return lax.dot_general(a, b, (((0,), (0,)), ((), ())), precision=HIGH, preferred_element_type=F32)
+def dot_nt(a, b):
+    return lax.dot_general(a, b, (((1,), (1,)), ((), ())), preferred_element_type=F32)
 
 
 def dot_nn(a, b):
@@ -123,16 +118,23 @@
     lags = lag_row((sx, sy, sz))
     lag_ref[...] = lags
     lane = lane_index()
-    gram = jnp.zeros((64, 128), F32)
-    pad = jnp.zeros((64, 256), F32)
+    gram = jnp.zeros((64, 64), F32)
     for piece in (u_up, u_both):
         for z in range(piece.shape[0]):
-            gram = gram + dot_nt(piece[z], jnp.concatenate([piece[z], pad], axis=0))
-    u_sums = jnp.where(lags < 64, pick(skewed(gram), lags), 0.0)
-    kept = keep[...].reshape(256, 256)
-    sent = swap[...].reshape(256, 256)
-    v_parts[:256], v_parts[256:] = halves(kept.T)
-    v_sums = pick(skewed(widened(dot_tn(kept, kept) + dot_tn(sent, sent))), lags)
+            high, low = halves(piece[z])
+            both = dot_nt(jnp.concatenate([high, low], axis=0), high)
+            gram = gram + both[:64] + both[64:] + dot_nt(high, low)
+    u_sums = jnp.where(lags < 64, pick(skewed(widened(gram)), lags), 0.0)
+    gram = jnp.zeros((256, 256), F32)
+    for piece in (keep, swap):
+        rows = piece[...].reshape(256, 256)
+        high, low = halves(rows)
+        t_high, t_low = halves(rows.T)
+        gram = gram + dot_nn(t_high, high) + dot_nn(t_low, high) + dot_nn(t_high, low)
+        if piece is keep:
+            v_parts[:256] = t_high
+            v_parts[256:] = t_low
+    v_sums = pick(skewed(widened(gram)), lags)
     fetch.wait()
     planes = [w_ref[z] for z in range(8)]
     w_sums = jnp.zeros((8, 128), F32)
@@ -155,7 +157,7 @@
         a_high, a_low = halves(u_up[z] if z < UP else u_both[z - UP])
         b_high, b_low = halves(other_up[z] if z < UP else other_both[z - UP])
         u_parts[z] = jnp.concatenate([b_high, a_high, b_low, a_low], axis=0)
-        gram = gram + dot_nt(b_high, a_high, None) + dot_nt(b_low, a_high, None) + dot_nt(b_high, a_low, None)
+        gram = gram + dot_nt(b_high, a_high) + dot_nt(b_low, a_high) + dot_nt(b_high, a_low)
     counted = (lax.axis_index("c") == 1) & (lane_index() < 16) & (lags < 128)
     out_ref[...] = before[...] + jnp.where(counted, pick(skewed(widened(gram)), lags - 64), 0.0)
 
@@ -168,8 +170,8 @@
         total = jnp.zeros((128, 64), F32)
         for z in planes:
             high, low = halves(near[z - planes[0]])
-            both = dot_nt(parts[z], high, None)
-            total = total + both[:128] + both[128:] + dot_nt(parts[z, :128], low, None)
+            both = dot_nt(parts[z], high)
+            total = total + both[:128] + both[128:] + dot_nt(parts[z, :128], low)
         sums.append(total)
     up, mixed = sums
     far = jnp.where(first, mixed[64:] + up[64:].T, (mixed[64:] + up[64:]).T)

time: 44.3 us -> 44.3 us (level)
  transfers between devices with their start and end apart: 6 -> 6, of which waited for: 1 -> 1; matrix products, arithmetic and copies ran while one was open for 0% -> 0% of each run, Pallas kernels for 10% -> 9%
where the time goes in v7:
time: 44.3 us; the launch traced here: 44.1 us
  blocking collectives  24.4 us (55%)
  starting transfers between devices  10.4 us (23%)
  Pallas kernels  6.49 us (15%)
  waiting for transfers between devices  2.75 us (6%)
    all_to_all x1, blocking collectives, local(): rows = near(lax.all_to_all(rows, SERVED, 0, 0, tiled=True))  24.4 us
    ppermute x6, starting transfers between devices, send(): return near(lax.ppermute(value, AXES, pairs))  10.4 us
    pallas_call x6, Pallas kernels, call(): pl.pallas_call(kernel, out_shape=out, in_specs=places, out_specs=specs, c...  6.49 us
    ppermute x6, waiting for transfers between devices, send(): return near(lax.ppermute(value, AXES, pairs))  2.75 us
  transfers between devices with their start and end apart: 6, of which 1 were waited for; matrix products, arithmetic and copies ran while one was open for 0% of the time, Pallas kernels for 9%

profile of v7, /device:TPU:1, one launch (start us, length us, event | category | flops | bytes accessed | tf_op | source)
XLA Modules:
  0.0 44.1 jit_solution(18109431038454914980)
XLA Ops:
  0.0 1.3 %shard_map.64 = (f32[3,64,256]{2,1,0:T(8,128)S(1)}, f32[5,64,256]{2,1,0:T(8,128)S(1)}, f32[4,64,256]{2,1,0:T(8,128)S(1)}, f32[4,64,256]{2,1,0:T(8,128)S(1)}) custom-call(f32[8,64,256]{2,1,0:T(8,128)} %u_ref.1, f32[8,64,256]{2,1,0:T(8,128)} %v_ref.1), custom_call_target="tpu_custom_call" | custom-call | tf_op jit(solution)/shard_map/pallas_call | solution.py:221
  1.3 3.3 %collective-permute-start.2 = (f32[3,64,256]{2,1,0:T(8,128)S(1)}, f32[3,64,256]{2,1,0:T(8,128)S(1)}, u32[]{:S(2)}, u32[]{:S(2)}) collective-permute-start(f32[3,64,256]{2,1,0:T(8,128)S(1)} %get-tuple-element.14.u_up), channel_id=1, source_target_pairs={{0,1},{1,0},{2,3},{3,2},{4,5},{5,4},{6,7},{7,6},{8,9},{9,8},{10,11... | collective-permute-start | bytes 589832 | tf_op jit(solution)/shard_map/ppermute | solution.py:233
  4.6 0.1 collective-permute-start.3
  4.7 0.0 collective-permute-start.5
  4.7 0.0 copy-start
  4.7 0.0 copy-start.2
  4.7 2.7 %collective-permute-start = (f32[4,64,256]{2,1,0:T(8,128)S(1)}, f32[4,64,256]{2,1,0:T(8,128)S(1)}, u32[]{:S(2)}, u32[]{:S(2)}) collective-permute-start(f32[4,64,256]{2,1,0:T(8,128)S(1)} %get-tuple-element.17.swap), channel_id=1, source_target_pairs={{0,32},{1,33},{2,34},{3,35},{4,36},{5,37},{6,38},{7,39},{8,40},{9,... | collective-permute-start | bytes 786440 | tf_op jit(solution)/shard_map/ppermute | solution.py:233
  7.3 2.7 %collective-permute-start.1 = (f32[4,64,256]{2,1,0:T(8,128)S(1)}, f32[4,64,256]{2,1,0:T(8,128)S(1)}, u32[]{:S(2)}, u32[]{:S(2)}) collective-permute-start(f32[4,64,256]{2,1,0:T(8,128)S(1)} %get-tuple-element.16.keep), channel_id=1, source_target_pairs={{0,192},{1,193},{2,194},{3,195},{4,196},{5,197},{6,198},{7,199},{8... | collective-permute-start | bytes 786440 | tf_op jit(solution)/shard_map/ppermute | solution.py:233
  10.1 0.0 collective-permute-done.2.other_up
  10.1 1.6 %collective-permute-start.4 = (f32[3,64,256]{2,1,0:T(8,128)S(1)}, f32[3,64,256]{2,1,0:T(8,128)S(1)}, u32[]{:S(2)}, u32[]{:S(2)}) collective-permute-start(f32[3,64,256]{2,1,0:T(8,128)S(1)} %get-tuple-element.14.u_up), channel_id=1, source_target_pairs={{0,2},{1,3},{2,4},{3,5},{4,6},{5,7},{6,8},{7,9},{8,10},{9,11},{10,... | collective-permute-start | bytes 589832 | tf_op jit(solution)/shard_map/ppermute | solution.py:233
  11.7 0.0 copy-done
  11.7 0.0 copy-done.1
  11.7 0.0 copy-done.2
  11.7 2.4 %shard_map.65 = (s32[8,128]{1,0:T(8,128)S(1)}, f32[8,128]{1,0:T(8,128)S(1)}, bf16[512,256]{1,0:T(8,128)(2,1)S(1)}) custom-call(s32[16]{0:T(128)S(1)} %copy-done, s32[16]{0:T(128)S(1)} %copy-done.1, s32[16]{0:T(128)S(1)} %copy-done.2, f32[3,64,256]{2,1,0:T(8,128)S(1)} %get-tuple-element.14.u_up, f32[5,64,256]{2,1,0:T(8,128)S(1)} %get-tuple-element.15.u_both, ...), custom_call_target="tpu_custom_call" | custom-call | tf_op jit(solution)/shard_map/pallas_call | solution.py:221
  14.2 0.0 collective-permute-done.3.other_both
  14.2 0.6 %shard_map.66 = (f32[8,128]{1,0:T(8,128)S(1)}, bf16[8,256,256]{2,1,0:T(8,128)(2,1)S(1)}) custom-call(s32[8,128]{1,0:T(8,128)S(1)} %get-tuple-element.18.lag_ref, f32[3,64,256]{2,1,0:T(8,128)S(1)} %get-tuple-element.14.u_up, f32[5,64,256]{2,1,0:T(8,128)S(1)} %get-tuple-element.15.u_both, f32[3,64,256]{2,1,0:T(8,128)S(1)} %collective-permute-done.2.other_up, ...), custom_call_target="tpu_custom_call" | custom-call | tf_op jit(solution)/shard_map/pallas_call | solution.py:221
  14.7 2.7 %collective-permute-done.4.near_up = f32[3,64,256]{2,1,0:T(8,128)S(1)} collective-permute-done((f32[3,64,256]{2,1,0:T(8,128)S(1)}, f32[3,64,256]{2,1,0:T(8,128)S(1)}, u32[]{:S(2)}, u32[]{:S(2)}) %collective-permute-start.4) | collective-permute-done | bytes 196640 | tf_op jit(solution)/shard_map/ppermute | solution.py:233
  17.5 0.0 collective-permute-done.5.near_both
  17.5 0.9 %shard_map.67.before = f32[8,128]{1,0:T(8,128)S(1)} custom-call(s32[8,128]{1,0:T(8,128)S(1)} %get-tuple-element.18.lag_ref, bf16[8,256,256]{2,1,0:T(8,128)(2,1)S(1)} %get-tuple-element.21.parts, f32[3,64,256]{2,1,0:T(8,128)S(1)} %collective-permute-done.4.near_up, f32[5,64,256]{2,1,0:T(8,128)S(1)} %collective-permute-done.5.near_both, ...), custom_call_target="tpu_custom_call" | custom-call | tf_op jit(solution)/shard_map/pallas_call | solution.py:221
  18.4 0.0 collective-permute-done.other
  18.4 0.0 collective-permute-done.1.near
  18.4 0.6 %shard_map.68 = f32[256,128]{1,0:T(8,128)S(1)} custom-call(s32[8,128]{1,0:T(8,128)S(1)} %get-tuple-element.18.lag_ref, bf16[512,256]{1,0:T(8,128)(2,1)S(1)} %get-tuple-element.19.parts, f32[4,64,256]{2,1,0:T(8,128)S(1)} %collective-permute-done.other, f32[4,64,256]{2,1,0:T(8,128)S(1)} %collective-permute-done.1.near, f32[8,128]{1,0:T(8,128)S(1)} %shard_map.67.before), custom_call_target="tpu_custom_call" | custom-call | tf_op jit(solution)/shard_map/pallas_call | solution.py:221
  19.0 24.4 %all_to_all.11 = f32[256,1,128]{2,1,0:T(1,128)S(1)} all-to-all(f32[256,1,128]{2,1,0:T(1,128)S(1)} %bitcast.4), channel_id=1, replica_groups=mesh['y'=4,'xh'=2,'xl'=2,'z'=8,'c'=2] {'y','xh','xl','z','c'}, dimensions={0} | all-to-all | bytes 262144 | tf_op jit(solution)/shard_map/all_to_all | solution.py:258
  43.4 0.8 %shard_map.69 = f32[3,16]{1,0:T(4,128)} custom-call(f32[256,128]{1,0:T(8,128)S(1)} %bitcast.5), custom_call_target="tpu_custom_call" | custom-call | tf_op jit(solution)/shard_map/pallas_call | solution.py:221
  (1 shorter events, 0.0 us)
Async XLA Ops:
  1.3 8.8 %collective-permute-start.2 = (f32[3,64,256]{2,1,0:T(8,128)S(1)}, f32[3,64,256]{2,1,0:T(8,128)S(1)}, u32[]{:S(2)}, u32[]{:S(2)}) collective-permute-start(f32[3,64,256]{2,1,0:T(8,128)S(1)} %get-tuple-element.14.u_up), channel_id=1, source_target_pairs={{0,1},{1,0},{2,3},{3,2},{4,5},{5,4},{6,7},{7,6},{8,9},{9,8},{10,11... | collective-permute-start | bytes 589832 | tf_op jit(solution)/shard_map/ppermute | solution.py:233
  4.6 9.6 %collective-permute-start.3 = (f32[5,64,256]{2,1,0:T(8,128)S(1)}, f32[5,64,256]{2,1,0:T(8,128)S(1)}, u32[]{:S(2)}, u32[]{:S(2)}) collective-permute-start(f32[5,64,256]{2,1,0:T(8,128)S(1)} %get-tuple-element.15.u_both), channel_id=1, source_target_pairs={{0,1},{1,0},{2,3},{3,2},{4,5},{5,4},{6,7},{7,6},{8,9},{9,8},{10,11... | collective-permute-start | bytes 983048 | tf_op jit(solution)/shard_map/ppermute | solution.py:233
  4.7 12.8 %collective-permute-start.5 = (f32[5,64,256]{2,1,0:T(8,128)S(1)}, f32[5,64,256]{2,1,0:T(8,128)S(1)}, u32[]{:S(2)}, u32[]{:S(2)}) collective-permute-start(f32[5,64,256]{2,1,0:T(8,128)S(1)} %get-tuple-element.15.u_both), channel_id=1, source_target_pairs={{0,30},{1,3},{2,0},{3,5},{4,2},{5,7},{6,4},{7,9},{8,6},{9,11},{10,... | collective-permute-start | bytes 983048 | tf_op jit(solution)/shard_map/ppermute | solution.py:233
  4.7 7.1 %copy-start = (s32[16]{0:T(128)S(1)}, s32[16]{0:T(128)}, u32[]{:S(2)}) copy-start(s32[16]{0:T(128)} %sx.1) | copy-start | bytes 196
  4.7 7.1 %copy-start.1 = (s32[16]{0:T(128)S(1)}, s32[16]{0:T(128)}, u32[]{:S(2)}) copy-start(s32[16]{0:T(128)} %sy.1) | copy-start | bytes 196
  4.7 7.1 %copy-start.2 = (s32[16]{0:T(128)S(1)}, s32[16]{0:T(128)}, u32[]{:S(2)}) copy-start(s32[16]{0:T(128)} %sz.1) | copy-start | bytes 196
  4.7 13.7 %collective-permute-start = (f32[4,64,256]{2,1,0:T(8,128)S(1)}, f32[4,64,256]{2,1,0:T(8,128)S(1)}, u32[]{:S(2)}, u32[]{:S(2)}) collective-permute-start(f32[4,64,256]{2,1,0:T(8,128)S(1)} %get-tuple-element.17.swap), channel_id=1, source_target_pairs={{0,32},{1,33},{2,34},{3,35},{4,36},{5,37},{6,38},{7,39},{8,40},{9,... | collective-permute-start | bytes 786440 | tf_op jit(solution)/shard_map/ppermute | solution.py:233
  7.3 11.0 %collective-permute-start.1 = (f32[4,64,256]{2,1,0:T(8,128)S(1)}, f32[4,64,256]{2,1,0:T(8,128)S(1)}, u32[]{:S(2)}, u32[]{:S(2)}) collective-permute-start(f32[4,64,256]{2,1,0:T(8,128)S(1)} %get-tuple-element.16.keep), channel_id=1, source_target_pairs={{0,192},{1,193},{2,194},{3,195},{4,196},{5,197},{6,198},{7,199},{8... | collective-permute-start | bytes 786440 | tf_op jit(solution)/shard_map/ppermute | solution.py:233
  10.1 7.4 %collective-permute-start.4 = (f32[3,64,256]{2,1,0:T(8,128)S(1)}, f32[3,64,256]{2,1,0:T(8,128)S(1)}, u32[]{:S(2)}, u32[]{:S(2)}) collective-permute-start(f32[3,64,256]{2,1,0:T(8,128)S(1)} %get-tuple-element.14.u_up), channel_id=1, source_target_pairs={{0,2},{1,3},{2,4},{3,5},{4,6},{5,7},{6,8},{7,9},{8,10},{9,11},{10,... | collective-permute-start | bytes 589832 | tf_op jit(solution)/shard_map/ppermute | solution.py:233

commit v8 on v7

--- a/solution.py
+++ b/solution.py
@@ -162,18 +162,24 @@
     out_ref[...] = before[...] + jnp.where(counted, pick(skewed(widened(gram)), lags - 64), 0.0)
 
 
-def u_kernel(lag_ref, parts, near_up, near_both, before, out_ref):
+def chip_sums(parts, near, planes):
+    total = jnp.zeros((128, 64), F32)
+    for z in planes:
+        high, low = halves(near[z - planes[0]])
+        both = dot_nt(parts[z], high)
+        total = total + both[:128] + both[128:] + dot_nt(parts[z, :128], low)
+    return total
+
+
+def up_kernel(parts, near_up, out_ref):
+    out_ref[...] = chip_sums(parts, near_up, range(UP))
+
+
+def u_kernel(lag_ref, parts, up_ref, near_both, before, out_ref):
     lags = lag_ref[...]
     first = lax.axis_index("c") == 0
-    sums = []
-    for near, planes in ((near_up, range(UP)), (near_both, range(UP, 8))):
-        total = jnp.zeros((128, 64), F32)
-        for z in planes:
-            high, low = halves(near[z - planes[0]])
-            both = dot_nt(parts[z], high)
-            total = total + both[:128] + both[128:] + dot_nt(parts[z, :128], low)
-        sums.append(total)
-    up, mixed = sums
+    up = up_ref[...]
+    mixed = chip_sums(parts, near_both, range(UP, 8))
     far = jnp.where(first, mixed[64:] + up[64:].T, (mixed[64:] + up[64:]).T)
     next_to = jnp.where(first, mixed[:64], up[:64].T)
     i = lax.broadcasted_iota(jnp.int32, (64, 64), 0)
@@ -209,7 +215,7 @@
         out_ref[axis : axis + 1, :] = total[:, axis * 16 : axis * 16 + 16] / energy
 
 
-ROOM = {core_kernel: 12, split_kernel: 2, own_kernel: 16, u_kernel: 12, v_kernel: 12, end_kernel: 4}
+ROOM = {up_kernel: 8, core_kernel: 12, split_kernel: 2, own_kernel: 16, u_kernel: 12, v_kernel: 12, end_kernel: 4}
 SMEM = pl.BlockSpec(memory_space=pltpu.SMEM)
 VMEM = pl.BlockSpec(memory_space=pltpu.VMEM)
 
@@ -253,7 +259,8 @@
     lags, part, v_parts = map(near, call(own_kernel, outs, *args, places=places, scratch_shapes=scratch))
     outs = (row, pltpu.VMEM((8, 256, 256), BF16))
     part, u_parts = map(near, call(core_kernel, outs, lags, near(u_up), near(u_both), other_up, other_both, part))
-    part = call(u_kernel, row, lags, u_parts, up, both, part)
+    early = call(up_kernel, pltpu.VMEM((128, 64), F32), u_parts, up)
+    part = call(u_kernel, row, lags, u_parts, near(early), both, part)
     rows = call(v_kernel, pltpu.VMEM((256, 128), F32), lags, v_parts, v_other, v_near, near(part))
     rows = near(lax.all_to_all(rows, SERVED, 0, 0, tiled=True))
     return call(end_kernel, jax.ShapeDtypeStruct((3, 16), F32), rows)

time: 44.3 us -> 44.3 us (level)
    pallas_call x6 -> x7, Pallas kernels: 6.49 us -> 6.65 us  [call(): pl.pallas_call(kernel, out_shape=out, in_specs=places, out_specs=specs, c...]
where the time goes in v8:
time: 44.3 us; the launch traced here: 44.1 us
  blocking collectives  24.2 us (55%)
  starting transfers between devices  10.4 us (23%)
  Pallas kernels  6.65 us (15%)
  waiting for transfers between devices  2.75 us (6%)
    all_to_all x1, blocking collectives, local(): rows = near(lax.all_to_all(rows, SERVED, 0, 0, tiled=True))  24.2 us
    ppermute x6, starting transfers between devices, send(): return near(lax.ppermute(value, AXES, pairs))  10.4 us
    pallas_call x7, Pallas kernels, call(): pl.pallas_call(kernel, out_shape=out, in_specs=places, out_specs=specs, c...  6.65 us
    ppermute x6, waiting for transfers between devices, send(): return near(lax.ppermute(value, AXES, pairs))  2.75 us
  transfers between devices with their start and end apart: 6, of which 1 were waited for; matrix products, arithmetic and copies ran while one was open for 0% of the time, Pallas kernels for 9%

profile of v8, /device:TPU:1, one launch (start us, length us, event | category | flops | bytes accessed | tf_op | source)
XLA Modules:
  0.0 44.1 jit_solution(5887422305968936348)
XLA Ops:
  0.0 1.3 %shard_map.64 = (f32[3,64,256]{2,1,0:T(8,128)S(1)}, f32[5,64,256]{2,1,0:T(8,128)S(1)}, f32[4,64,256]{2,1,0:T(8,128)S(1)}, f32[4,64,256]{2,1,0:T(8,128)S(1)}) custom-call(f32[8,64,256]{2,1,0:T(8,128)} %u_ref.1, f32[8,64,256]{2,1,0:T(8,128)} %v_ref.1), custom_call_target="tpu_custom_call" | custom-call | tf_op jit(solution)/shard_map/pallas_call | solution.py:227
  1.3 3.3 %collective-permute-start.2 = (f32[3,64,256]{2,1,0:T(8,128)S(1)}, f32[3,64,256]{2,1,0:T(8,128)S(1)}, u32[]{:S(2)}, u32[]{:S(2)}) collective-permute-start(f32[3,64,256]{2,1,0:T(8,128)S(1)} %get-tuple-element.14.u_up), channel_id=1, source_target_pairs={{0,1},{1,0},{2,3},{3,2},{4,5},{5,4},{6,7},{7,6},{8,9},{9,8},{10,11... | collective-permute-start | bytes 589832 | tf_op jit(solution)/shard_map/ppermute | solution.py:239
  4.6 0.1 collective-permute-start.3
  4.7 0.0 collective-permute-start.5
  4.7 0.0 copy-start
  4.7 2.7 %collective-permute-start = (f32[4,64,256]{2,1,0:T(8,128)S(1)}, f32[4,64,256]{2,1,0:T(8,128)S(1)}, u32[]{:S(2)}, u32[]{:S(2)}) collective-permute-start(f32[4,64,256]{2,1,0:T(8,128)S(1)} %get-tuple-element.17.swap), channel_id=1, source_target_pairs={{0,32},{1,33},{2,34},{3,35},{4,36},{5,37},{6,38},{7,39},{8,40},{9,... | collective-permute-start | bytes 786440 | tf_op jit(solution)/shard_map/ppermute | solution.py:239
  7.3 2.7 %collective-permute-start.1 = (f32[4,64,256]{2,1,0:T(8,128)S(1)}, f32[4,64,256]{2,1,0:T(8,128)S(1)}, u32[]{:S(2)}, u32[]{:S(2)}) collective-permute-start(f32[4,64,256]{2,1,0:T(8,128)S(1)} %get-tuple-element.16.keep), channel_id=1, source_target_pairs={{0,192},{1,193},{2,194},{3,195},{4,196},{5,197},{6,198},{7,199},{8... | collective-permute-start | bytes 786440 | tf_op jit(solution)/shard_map/ppermute | solution.py:239
  10.1 0.0 collective-permute-done.2.other_up
  10.1 1.6 %collective-permute-start.4 = (f32[3,64,256]{2,1,0:T(8,128)S(1)}, f32[3,64,256]{2,1,0:T(8,128)S(1)}, u32[]{:S(2)}, u32[]{:S(2)}) collective-permute-start(f32[3,64,256]{2,1,0:T(8,128)S(1)} %get-tuple-element.14.u_up), channel_id=1, source_target_pairs={{0,2},{1,3},{2,4},{3,5},{4,6},{5,7},{6,8},{7,9},{8,10},{9,11},{10,... | collective-permute-start | bytes 589832 | tf_op jit(solution)/shard_map/ppermute | solution.py:239
  11.7 0.0 copy-done
  11.7 0.0 copy-done.1
  11.7 0.0 copy-done.2
  11.7 2.4 %shard_map.65 = (s32[8,128]{1,0:T(8,128)S(1)}, f32[8,128]{1,0:T(8,128)S(1)}, bf16[512,256]{1,0:T(8,128)(2,1)S(1)}) custom-call(s32[16]{0:T(128)S(1)} %copy-done, s32[16]{0:T(128)S(1)} %copy-done.1, s32[16]{0:T(128)S(1)} %copy-done.2, f32[3,64,256]{2,1,0:T(8,128)S(1)} %get-tuple-element.14.u_up, f32[5,64,256]{2,1,0:T(8,128)S(1)} %get-tuple-element.15.u_both, ...), custom_call_target="tpu_custom_call" | custom-call | tf_op jit(solution)/shard_map/pallas_call | solution.py:227
  14.2 0.0 collective-permute-done.3.other_both
  14.2 0.6 %shard_map.66 = (f32[8,128]{1,0:T(8,128)S(1)}, bf16[8,256,256]{2,1,0:T(8,128)(2,1)S(1)}) custom-call(s32[8,128]{1,0:T(8,128)S(1)} %get-tuple-element.18.lag_ref, f32[3,64,256]{2,1,0:T(8,128)S(1)} %get-tuple-element.14.u_up, f32[5,64,256]{2,1,0:T(8,128)S(1)} %get-tuple-element.15.u_both, f32[3,64,256]{2,1,0:T(8,128)S(1)} %collective-permute-done.2.other_up, ...), custom_call_target="tpu_custom_call" | custom-call | tf_op jit(solution)/shard_map/pallas_call | solution.py:227
  14.7 2.7 %collective-permute-done.4.near_up = f32[3,64,256]{2,1,0:T(8,128)S(1)} collective-permute-done((f32[3,64,256]{2,1,0:T(8,128)S(1)}, f32[3,64,256]{2,1,0:T(8,128)S(1)}, u32[]{:S(2)}, u32[]{:S(2)}) %collective-permute-start.4) | collective-permute-done | bytes 196640 | tf_op jit(solution)/shard_map/ppermute | solution.py:239
  17.5 0.3 shard_map.67.up_ref
  17.8 0.0 collective-permute-done.5.near_both
  17.8 0.7 %shard_map.68.before = f32[8,128]{1,0:T(8,128)S(1)} custom-call(s32[8,128]{1,0:T(8,128)S(1)} %get-tuple-element.18.lag_ref, bf16[8,256,256]{2,1,0:T(8,128)(2,1)S(1)} %get-tuple-element.21.parts, f32[128,64]{1,0:T(8,128)S(1)} %shard_map.67.up_ref, f32[5,64,256]{2,1,0:T(8,128)S(1)} %collective-permute-done.5.near_both, f32[8,128]{1,0:T(8,128)S(1)} %get-tuple-element.22.before), custom_call_target="tpu_custom_call" | custom-call | tf_op jit(solution)/shard_map/pallas_call | solution.py:227
  18.5 0.0 collective-permute-done.other
  18.5 0.0 collective-permute-done.1.near
  18.5 0.6 %shard_map.69 = f32[256,128]{1,0:T(8,128)S(1)} custom-call(s32[8,128]{1,0:T(8,128)S(1)} %get-tuple-element.18.lag_ref, bf16[512,256]{1,0:T(8,128)(2,1)S(1)} %get-tuple-element.19.parts, f32[4,64,256]{2,1,0:T(8,128)S(1)} %collective-permute-done.other, f32[4,64,256]{2,1,0:T(8,128)S(1)} %collective-permute-done.1.near, f32[8,128]{1,0:T(8,128)S(1)} %shard_map.68.before), custom_call_target="tpu_custom_call" | custom-call | tf_op jit(solution)/shard_map/pallas_call | solution.py:227
  19.1 24.2 %all_to_all.11 = f32[256,1,128]{2,1,0:T(1,128)S(1)} all-to-all(f32[256,1,128]{2,1,0:T(1,128)S(1)} %bitcast.4), channel_id=1, replica_groups=mesh['y'=4,'xh'=2,'xl'=2,'z'=8,'c'=2] {'y','xh','xl','z','c'}, dimensions={0} | all-to-all | bytes 262144 | tf_op jit(solution)/shard_map/all_to_all | solution.py:265
  43.4 0.8 %shard_map.70 = f32[3,16]{1,0:T(4,128)} custom-call(f32[256,128]{1,0:T(8,128)S(1)} %bitcast.5), custom_call_target="tpu_custom_call" | custom-call | tf_op jit(solution)/shard_map/pallas_call | solution.py:227
  (2 shorter events, 0.0 us)
Async XLA Ops:
  1.3 8.8 %collective-permute-start.2 = (f32[3,64,256]{2,1,0:T(8,128)S(1)}, f32[3,64,256]{2,1,0:T(8,128)S(1)}, u32[]{:S(2)}, u32[]{:S(2)}) collective-permute-start(f32[3,64,256]{2,1,0:T(8,128)S(1)} %get-tuple-element.14.u_up), channel_id=1, source_target_pairs={{0,1},{1,0},{2,3},{3,2},{4,5},{5,4},{6,7},{7,6},{8,9},{9,8},{10,11... | collective-permute-start | bytes 589832 | tf_op jit(solution)/shard_map/ppermute | solution.py:239
  4.6 9.6 %collective-permute-start.3 = (f32[5,64,256]{2,1,0:T(8,128)S(1)}, f32[5,64,256]{2,1,0:T(8,128)S(1)}, u32[]{:S(2)}, u32[]{:S(2)}) collective-permute-start(f32[5,64,256]{2,1,0:T(8,128)S(1)} %get-tuple-element.15.u_both), channel_id=1, source_target_pairs={{0,1},{1,0},{2,3},{3,2},{4,5},{5,4},{6,7},{7,6},{8,9},{9,8},{10,11... | collective-permute-start | bytes 983048 | tf_op jit(solution)/shard_map/ppermute | solution.py:239
  4.7 13.1 %collective-permute-start.5 = (f32[5,64,256]{2,1,0:T(8,128)S(1)}, f32[5,64,256]{2,1,0:T(8,128)S(1)}, u32[]{:S(2)}, u32[]{:S(2)}) collective-permute-start(f32[5,64,256]{2,1,0:T(8,128)S(1)} %get-tuple-element.15.u_both), channel_id=1, source_target_pairs={{0,30},{1,3},{2,0},{3,5},{4,2},{5,7},{6,4},{7,9},{8,6},{9,11},{10,... | collective-permute-start | bytes 983048 | tf_op jit(solution)/shard_map/ppermute | solution.py:239
  4.7 7.1 %copy-start = (s32[16]{0:T(128)S(1)}, s32[16]{0:T(128)}, u32[]{:S(2)}) copy-start(s32[16]{0:T(128)} %sx.1) | copy-start | bytes 196
  4.7 7.1 %copy-start.1 = (s32[16]{0:T(128)S(1)}, s32[16]{0:T(128)}, u32[]{:S(2)}) copy-start(s32[16]{0:T(128)} %sy.1) | copy-start | bytes 196
  4.7 7.1 %copy-start.2 = (s32[16]{0:T(128)S(1)}, s32[16]{0:T(128)}, u32[]{:S(2)}) copy-start(s32[16]{0:T(128)} %sz.1) | copy-start | bytes 196
  4.7 13.9 %collective-permute-start = (f32[4,64,256]{2,1,0:T(8,128)S(1)}, f32[4,64,256]{2,1,0:T(8,128)S(1)}, u32[]{:S(2)}, u32[]{:S(2)}) collective-permute-start(f32[4,64,256]{2,1,0:T(8,128)S(1)} %get-tuple-element.17.swap), channel_id=1, source_target_pairs={{0,32},{1,33},{2,34},{3,35},{4,36},{5,37},{6,38},{7,39},{8,40},{9,... | collective-permute-start | bytes 786440 | tf_op jit(solution)/shard_map/ppermute | solution.py:239
  7.3 11.2 %collective-permute-start.1 = (f32[4,64,256]{2,1,0:T(8,128)S(1)}, f32[4,64,256]{2,1,0:T(8,128)S(1)}, u32[]{:S(2)}, u32[]{:S(2)}) collective-permute-start(f32[4,64,256]{2,1,0:T(8,128)S(1)} %get-tuple-element.16.keep), channel_id=1, source_target_pairs={{0,192},{1,193},{2,194},{3,195},{4,196},{5,197},{6,198},{7,199},{8... | collective-permute-start | bytes 786440 | tf_op jit(solution)/shard_map/ppermute | solution.py:239
  10.1 7.4 %collective-permute-start.4 = (f32[3,64,256]{2,1,0:T(8,128)S(1)}, f32[3,64,256]{2,1,0:T(8,128)S(1)}, u32[]{:S(2)}, u32[]{:S(2)}) collective-permute-start(f32[3,64,256]{2,1,0:T(8,128)S(1)} %get-tuple-element.14.u_up), channel_id=1, source_target_pairs={{0,2},{1,3},{2,4},{3,5},{4,6},{5,7},{6,8},{7,9},{8,10},{9,11},{10,... | collective-permute-start | bytes 589832 | tf_op jit(solution)/shard_map/ppermute | solution.py:239

commit v9 on v8

--- a/solution.py
+++ b/solution.py
@@ -172,7 +172,7 @@
 
 
 def up_kernel(parts, near_up, out_ref):
-    out_ref[...] = chip_sums(parts, near_up, range(UP))
+    out_ref[...] = chip_sums(parts, near_up, range(UP)).T
 
 
 def u_kernel(lag_ref, parts, up_ref, near_both, before, out_ref):
@@ -180,8 +180,8 @@
     first = lax.axis_index("c") == 0
     up = up_ref[...]
     mixed = chip_sums(parts, near_both, range(UP, 8))
-    far = jnp.where(first, mixed[64:] + up[64:].T, (mixed[64:] + up[64:]).T)
-    next_to = jnp.where(first, mixed[:64], up[:64].T)
+    far = jnp.where(first, mixed[64:], mixed[64:].T) + up[:, 64:]
+    next_to = jnp.where(first, mixed[:64], up[:, :64])
     i = lax.broadcasted_iota(jnp.int32, (64, 64), 0)
     j = lax.broadcasted_iota(jnp.int32, (64, 64), 1)
     gram = jnp.concatenate([next_to, jnp.where(j <= i, far, 0.0)], axis=1)
@@ -259,7 +259,7 @@
     lags, part, v_parts = map(near, call(own_kernel, outs, *args, places=places, scratch_shapes=scratch))
     outs = (row, pltpu.VMEM((8, 256, 256), BF16))
     part, u_parts = map(near, call(core_kernel, outs, lags, near(u_up), near(u_both), other_up, other_both, part))
-    early = call(up_kernel, pltpu.VMEM((128, 64), F32), u_parts, up)
+    early = call(up_kernel, pltpu.VMEM((64, 128), F32), u_parts, up)
     part = call(u_kernel, row, lags, u_parts, near(early), both, part)
     rows = call(v_kernel, pltpu.VMEM((256, 128), F32), lags, v_parts, v_other, v_near, near(part))
     rows = near(lax.all_to_all(rows, SERVED, 0, 0, tiled=True))

time: 44.3 us -> 44.3 us (level)
  no operation moved by 1% of the time
where the time goes in v9:
time: 44.3 us; the launch traced here: 44.1 us
  blocking collectives  24.2 us (55%)
  starting transfers between devices  10.4 us (23%)
  Pallas kernels  6.67 us (15%)
  waiting for transfers between devices  2.76 us (6%)
    all_to_all x1, blocking collectives, local(): rows = near(lax.all_to_all(rows, SERVED, 0, 0, tiled=True))  24.2 us
    ppermute x6, starting transfers between devices, send(): return near(lax.ppermute(value, AXES, pairs))  10.4 us
    pallas_call x7, Pallas kernels, call(): pl.pallas_call(kernel, out_shape=out, in_specs=places, out_specs=specs, c...  6.67 us
    ppermute x6, waiting for transfers between devices, send(): return near(lax.ppermute(value, AXES, pairs))  2.76 us
  transfers between devices with their start and end apart: 6, of which 1 were waited for; matrix products, arithmetic and copies ran while one was open for 0% of the time, Pallas kernels for 9%

profile of v9, /device:TPU:1, one launch (start us, length us, event | category | flops | bytes accessed | tf_op | source)
XLA Modules:
  0.0 44.1 jit_solution(57904048706755319)
XLA Ops:
  0.0 1.3 %shard_map.64 = (f32[3,64,256]{2,1,0:T(8,128)S(1)}, f32[5,64,256]{2,1,0:T(8,128)S(1)}, f32[4,64,256]{2,1,0:T(8,128)S(1)}, f32[4,64,256]{2,1,0:T(8,128)S(1)}) custom-call(f32[8,64,256]{2,1,0:T(8,128)} %u_ref.1, f32[8,64,256]{2,1,0:T(8,128)} %v_ref.1), custom_call_target="tpu_custom_call" | custom-call | tf_op jit(solution)/shard_map/pallas_call | solution.py:227
  1.3 3.3 %collective-permute-start.2 = (f32[3,64,256]{2,1,0:T(8,128)S(1)}, f32[3,64,256]{2,1,0:T(8,128)S(1)}, u32[]{:S(2)}, u32[]{:S(2)}) collective-permute-start(f32[3,64,256]{2,1,0:T(8,128)S(1)} %get-tuple-element.14.u_up), channel_id=1, source_target_pairs={{0,1},{1,0},{2,3},{3,2},{4,5},{5,4},{6,7},{7,6},{8,9},{9,8},{10,11... | collective-permute-start | bytes 589832 | tf_op jit(solution)/shard_map/ppermute | solution.py:239
  4.6 0.1 collective-permute-start.3
  4.7 0.0 collective-permute-start.5
  4.7 0.0 copy-start
  4.7 2.7 %collective-permute-start = (f32[4,64,256]{2,1,0:T(8,128)S(1)}, f32[4,64,256]{2,1,0:T(8,128)S(1)}, u32[]{:S(2)}, u32[]{:S(2)}) collective-permute-start(f32[4,64,256]{2,1,0:T(8,128)S(1)} %get-tuple-element.17.swap), channel_id=1, source_target_pairs={{0,32},{1,33},{2,34},{3,35},{4,36},{5,37},{6,38},{7,39},{8,40},{9,... | collective-permute-start | bytes 786440 | tf_op jit(solution)/shard_map/ppermute | solution.py:239
  7.3 2.7 %collective-permute-start.1 = (f32[4,64,256]{2,1,0:T(8,128)S(1)}, f32[4,64,256]{2,1,0:T(8,128)S(1)}, u32[]{:S(2)}, u32[]{:S(2)}) collective-permute-start(f32[4,64,256]{2,1,0:T(8,128)S(1)} %get-tuple-element.16.keep), channel_id=1, source_target_pairs={{0,192},{1,193},{2,194},{3,195},{4,196},{5,197},{6,198},{7,199},{8... | collective-permute-start | bytes 786440 | tf_op jit(solution)/shard_map/ppermute | solution.py:239
  10.1 0.0 collective-permute-done.2.other_up
  10.1 1.6 %collective-permute-start.4 = (f32[3,64,256]{2,1,0:T(8,128)S(1)}, f32[3,64,256]{2,1,0:T(8,128)S(1)}, u32[]{:S(2)}, u32[]{:S(2)}) collective-permute-start(f32[3,64,256]{2,1,0:T(8,128)S(1)} %get-tuple-element.14.u_up), channel_id=1, source_target_pairs={{0,2},{1,3},{2,4},{3,5},{4,6},{5,7},{6,8},{7,9},{8,10},{9,11},{10,... | collective-permute-start | bytes 589832 | tf_op jit(solution)/shard_map/ppermute | solution.py:239
  11.7 0.0 copy-done
  11.7 0.0 copy-done.1
  11.7 0.0 copy-done.2
  11.7 2.4 %shard_map.65 = (s32[8,128]{1,0:T(8,128)S(1)}, f32[8,128]{1,0:T(8,128)S(1)}, bf16[512,256]{1,0:T(8,128)(2,1)S(1)}) custom-call(s32[16]{0:T(128)S(1)} %copy-done, s32[16]{0:T(128)S(1)} %copy-done.1, s32[16]{0:T(128)S(1)} %copy-done.2, f32[3,64,256]{2,1,0:T(8,128)S(1)} %get-tuple-element.14.u_up, f32[5,64,256]{2,1,0:T(8,128)S(1)} %get-tuple-element.15.u_both, ...), custom_call_target="tpu_custom_call" | custom-call | tf_op jit(solution)/shard_map/pallas_call | solution.py:227
  14.2 0.0 collective-permute-done.3.other_both
  14.2 0.6 %shard_map.66 = (f32[8,128]{1,0:T(8,128)S(1)}, bf16[8,256,256]{2,1,0:T(8,128)(2,1)S(1)}) custom-call(s32[8,128]{1,0:T(8,128)S(1)} %get-tuple-element.18.lag_ref, f32[3,64,256]{2,1,0:T(8,128)S(1)} %get-tuple-element.14.u_up, f32[5,64,256]{2,1,0:T(8,128)S(1)} %get-tuple-element.15.u_both, f32[3,64,256]{2,1,0:T(8,128)S(1)} %collective-permute-done.2.other_up, ...), custom_call_target="tpu_custom_call" | custom-call | tf_op jit(solution)/shard_map/pallas_call | solution.py:227
  14.7 2.7 %collective-permute-done.4.near_up = f32[3,64,256]{2,1,0:T(8,128)S(1)} collective-permute-done((f32[3,64,256]{2,1,0:T(8,128)S(1)}, f32[3,64,256]{2,1,0:T(8,128)S(1)}, u32[]{:S(2)}, u32[]{:S(2)}) %collective-permute-start.4) | collective-permute-done | bytes 196640 | tf_op jit(solution)/shard_map/ppermute | solution.py:239
  17.5 0.4 shard_map.67.up_ref
  17.8 0.0 collective-permute-done.5.near_both
  17.8 0.7 %shard_map.68.before = f32[8,128]{1,0:T(8,128)S(1)} custom-call(s32[8,128]{1,0:T(8,128)S(1)} %get-tuple-element.18.lag_ref, bf16[8,256,256]{2,1,0:T(8,128)(2,1)S(1)} %get-tuple-element.21.parts, f32[64,128]{1,0:T(8,128)S(1)} %shard_map.67.up_ref, f32[5,64,256]{2,1,0:T(8,128)S(1)} %collective-permute-done.5.near_both, f32[8,128]{1,0:T(8,128)S(1)} %get-tuple-element.22.before), custom_call_target="tpu_custom_call" | custom-call | tf_op jit(solution)/shard_map/pallas_call | solution.py:227
  18.5 0.0 collective-permute-done.other
  18.5 0.0 collective-permute-done.1.near
  18.6 0.6 %shard_map.69 = f32[256,128]{1,0:T(8,128)S(1)} custom-call(s32[8,128]{1,0:T(8,128)S(1)} %get-tuple-element.18.lag_ref, bf16[512,256]{1,0:T(8,128)(2,1)S(1)} %get-tuple-element.19.parts, f32[4,64,256]{2,1,0:T(8,128)S(1)} %collective-permute-done.other, f32[4,64,256]{2,1,0:T(8,128)S(1)} %collective-permute-done.1.near, f32[8,128]{1,0:T(8,128)S(1)} %shard_map.68.before), custom_call_target="tpu_custom_call" | custom-call | tf_op jit(solution)/shard_map/pallas_call | solution.py:227
  19.2 24.2 %all_to_all.11 = f32[256,1,128]{2,1,0:T(1,128)S(1)} all-to-all(f32[256,1,128]{2,1,0:T(1,128)S(1)} %bitcast.4), channel_id=1, replica_groups=mesh['y'=4,'xh'=2,'xl'=2,'z'=8,'c'=2] {'y','xh','xl','z','c'}, dimensions={0} | all-to-all | bytes 262144 | tf_op jit(solution)/shard_map/all_to_all | solution.py:265
  43.4 0.8 %shard_map.70 = f32[3,16]{1,0:T(4,128)} custom-call(f32[256,128]{1,0:T(8,128)S(1)} %bitcast.5), custom_call_target="tpu_custom_call" | custom-call | tf_op jit(solution)/shard_map/pallas_call | solution.py:227
  (2 shorter events, 0.0 us)
Async XLA Ops:
  1.3 8.8 %collective-permute-start.2 = (f32[3,64,256]{2,1,0:T(8,128)S(1)}, f32[3,64,256]{2,1,0:T(8,128)S(1)}, u32[]{:S(2)}, u32[]{:S(2)}) collective-permute-start(f32[3,64,256]{2,1,0:T(8,128)S(1)} %get-tuple-element.14.u_up), channel_id=1, source_target_pairs={{0,1},{1,0},{2,3},{3,2},{4,5},{5,4},{6,7},{7,6},{8,9},{9,8},{10,11... | collective-permute-start | bytes 589832 | tf_op jit(solution)/shard_map/ppermute | solution.py:239
  4.6 9.6 %collective-permute-start.3 = (f32[5,64,256]{2,1,0:T(8,128)S(1)}, f32[5,64,256]{2,1,0:T(8,128)S(1)}, u32[]{:S(2)}, u32[]{:S(2)}) collective-permute-start(f32[5,64,256]{2,1,0:T(8,128)S(1)} %get-tuple-element.15.u_both), channel_id=1, source_target_pairs={{0,1},{1,0},{2,3},{3,2},{4,5},{5,4},{6,7},{7,6},{8,9},{9,8},{10,11... | collective-permute-start | bytes 983048 | tf_op jit(solution)/shard_map/ppermute | solution.py:239
  4.7 13.2 %collective-permute-start.5 = (f32[5,64,256]{2,1,0:T(8,128)S(1)}, f32[5,64,256]{2,1,0:T(8,128)S(1)}, u32[]{:S(2)}, u32[]{:S(2)}) collective-permute-start(f32[5,64,256]{2,1,0:T(8,128)S(1)} %get-tuple-element.15.u_both), channel_id=1, source_target_pairs={{0,30},{1,3},{2,0},{3,5},{4,2},{5,7},{6,4},{7,9},{8,6},{9,11},{10,... | collective-permute-start | bytes 983048 | tf_op jit(solution)/shard_map/ppermute | solution.py:239
  4.7 7.1 %copy-start = (s32[16]{0:T(128)S(1)}, s32[16]{0:T(128)}, u32[]{:S(2)}) copy-start(s32[16]{0:T(128)} %sx.1) | copy-start | bytes 196
  4.7 7.1 %copy-start.1 = (s32[16]{0:T(128)S(1)}, s32[16]{0:T(128)}, u32[]{:S(2)}) copy-start(s32[16]{0:T(128)} %sy.1) | copy-start | bytes 196
  4.7 7.1 %copy-start.2 = (s32[16]{0:T(128)S(1)}, s32[16]{0:T(128)}, u32[]{:S(2)}) copy-start(s32[16]{0:T(128)} %sz.1) | copy-start | bytes 196
  4.7 13.9 %collective-permute-start = (f32[4,64,256]{2,1,0:T(8,128)S(1)}, f32[4,64,256]{2,1,0:T(8,128)S(1)}, u32[]{:S(2)}, u32[]{:S(2)}) collective-permute-start(f32[4,64,256]{2,1,0:T(8,128)S(1)} %get-tuple-element.17.swap), channel_id=1, source_target_pairs={{0,32},{1,33},{2,34},{3,35},{4,36},{5,37},{6,38},{7,39},{8,40},{9,... | collective-permute-start | bytes 786440 | tf_op jit(solution)/shard_map/ppermute | solution.py:239
  7.3 11.2 %collective-permute-start.1 = (f32[4,64,256]{2,1,0:T(8,128)S(1)}, f32[4,64,256]{2,1,0:T(8,128)S(1)}, u32[]{:S(2)}, u32[]{:S(2)}) collective-permute-start(f32[4,64,256]{2,1,0:T(8,128)S(1)} %get-tuple-element.16.keep), channel_id=1, source_target_pairs={{0,192},{1,193},{2,194},{3,195},{4,196},{5,197},{6,198},{7,199},{8... | collective-permute-start | bytes 786440 | tf_op jit(solution)/shard_map/ppermute | solution.py:239
  10.1 7.4 %collective-permute-start.4 = (f32[3,64,256]{2,1,0:T(8,128)S(1)}, f32[3,64,256]{2,1,0:T(8,128)S(1)}, u32[]{:S(2)}, u32[]{:S(2)}) collective-permute-start(f32[3,64,256]{2,1,0:T(8,128)S(1)} %get-tuple-element.14.u_up), channel_id=1, source_target_pairs={{0,2},{1,3},{2,4},{3,5},{4,6},{5,7},{6,8},{7,9},{8,10},{9,11},{10,... | collective-permute-start | bytes 589832 | tf_op jit(solution)/shard_map/ppermute | solution.py:239
